TPU v7x, 256 devices: a whole 4x4x8 slice. The times are simulated.
256 devices in a mesh: blk: 128 (over x, z, y), rep: 2 (over core).
Axes of the slice: x: 4, y: 4, z: 8, core: 2. Of those that a mesh axis runs over, the one named last changes fastest.
Arguments:
- item_factors: bfloat16 [262144, 256], P('blk')
- user_factors: float32 [2048, 256], P(('blk', 'rep'))
- item_lists: int32 [2048, 128], P(('blk', 'rep')), may hold values from 0 to 262143, as said below
- counts: int32 [2048], P(('blk', 'rep')), may hold values from 16 to 112, as said below
- plays: int32 [2048, 128], P(('blk', 'rep')), may hold values from 0 to 999
Outputs:
- new_factors: float32 [2048, 256], P(('blk', 'rep'))
- residual_norms: float32 [4], replicated
Inputs may be any that keep to these rules, and one draw needn't show every extreme that they name: `item_lists`: entries are global item rows; index b of blk holds rows b * 2048 to (b + 1) * 2048 - 1. Among the live slots of the users of one device, at most 8 name rows held by one index of blk, and in every draw some index of blk is named by exactly 8 live slots of every device. The padding slots of one device name rows of every index of blk exactly 4 times. Slots at or after counts[u] are padding. The 8 users of one device have 8 * 64 live slots in all.
All inputs are finite; a program needn't handle non-finite values.
Results may differ from a plain program's by a relative error of at most 0.0003.
Values may be sent and summed in bfloat16 or wider, within the bound.
A program may use at most 64 MiB of HBM per device.

v0:
```python
import jax
import jax.numpy as jnp
from jax import lax
from jax.sharding import Mesh
from jax.sharding import PartitionSpec as P

ITERS = 3
BLK_REP = ("blk_0", "blk_1", "blk_2", "rep")
BLK = ("blk_0", "blk_1", "blk_2")


conf_scale = 40.0
ridge = 1.0
tiny = 1e-06


def over_axes(array, axes):
    for axis in axes:
        array = lax.psum(array, axis)
    return array


def split_up(array, dim, devices):
    dims = array.shape
    pieces = array.reshape(*dims[:dim], devices, dims[dim] // devices, *dims[dim + 1 :])
    return jnp.moveaxis(pieces, dim, 0)


def laid_out(pieces, dim):
    dims = list(pieces.shape[1:])
    dims[dim] *= pieces.shape[0]
    return jnp.moveaxis(pieces, 0, dim).reshape(dims)


def moved_by_axis(pieces, axes, sequence):
    dims = [lax.axis_size(a) for a in axes]
    pieces = pieces.reshape(*dims, *pieces.shape[1:])
    for k in sequence:
        pieces = lax.all_to_all(pieces, axes[k], split_axis=k, concat_axis=k, tiled=True)
    return pieces.reshape(-1, *pieces.shape[len(axes) :])


def exchange_by_axis(array, axes, sequence, split_dim, concat_dim):
    pieces = split_up(array, split_dim, lax.axis_size(axes))
    return laid_out(moved_by_axis(pieces, axes, sequence), concat_dim)


def operator_apply(vector, gram, item_rows, extra_weight):
    along = jnp.einsum(
        "ulk,uk->ul",
        item_rows,
        vector,
        precision=lax.Precision.HIGHEST,
        preferred_element_type=jnp.float32,
    )
    back = jnp.einsum(
        "ul,ulk->uk",
        extra_weight * along,
        item_rows,
        precision=lax.Precision.HIGHEST,
        preferred_element_type=jnp.float32,
    )
    return jnp.dot(vector, gram, precision=lax.Precision.HIGHEST) + back + ridge * vector


def global_squares(value):
    return over_axes(value, BLK_REP)


def pack_requests(owner_key, local, blocks, capacity):
    slot_total = owner_key.shape[0]
    order = jnp.argsort(owner_key, stable=True)
    sorted_owner = owner_key[order]
    starts = jnp.searchsorted(sorted_owner, jnp.arange(blocks + 1, dtype=jnp.int32))
    rank_sorted = jnp.arange(slot_total, dtype=jnp.int32) - starts[sorted_owner]
    place_sorted = jnp.where(
        sorted_owner < blocks, sorted_owner * capacity + rank_sorted, blocks * capacity
    )
    place = jnp.zeros((slot_total,), jnp.int32).at[order].set(place_sorted)
    requests = jnp.zeros((blocks * capacity + 1,), jnp.int32).at[place].set(local)
    requests = requests[: blocks * capacity].reshape(blocks, capacity)
    return (requests, jnp.minimum(place, blocks * capacity - 1))


def body(item_factors, user_factors, item_lists, counts, plays):
    own_rows, width = item_factors.shape
    user_count, list_len = item_lists.shape
    blocks = lax.axis_size(BLK)
    slot_total = user_count * list_len
    half_rows = own_rows // lax.axis_size("rep")
    mine = lax.dynamic_slice_in_dim(item_factors, lax.axis_index("rep") * half_rows, half_rows, 0)
    partial_gram = lax.dot_general(
        mine, mine, (((0,), (0,)), ((), ())), preferred_element_type=jnp.float32
    )
    gram = over_axes(partial_gram, BLK_REP)
    live = jnp.arange(list_len, dtype=jnp.int32)[None, :] < counts[:, None]
    flat_ids = item_lists.reshape(slot_total)
    owner = flat_ids // own_rows
    local = flat_ids % own_rows
    capacity = 3 * slot_total // (2 * blocks)
    requests, place = pack_requests(owner, local, blocks, capacity)
    found = item_factors[exchange_by_axis(requests, BLK, (0, 1, 2), 0, 0)]
    reply = lax.all_to_all(found, BLK, split_axis=0, concat_axis=0, tiled=True)
    item_rows = reply.reshape(blocks * capacity, width)[place].reshape(user_count, list_len, width)
    confidence = 1.0 + conf_scale * jnp.log(2.0 + plays.astype(jnp.float32))
    full_weight = jnp.where(live, confidence, jnp.float32(0.0))
    extra_weight = jnp.where(live, confidence - 1.0, jnp.float32(0.0))
    target = jnp.einsum(
        "ul,ulk->uk",
        full_weight,
        item_rows,
        precision=lax.Precision.HIGHEST,
        preferred_element_type=jnp.float32,
    )
    solution = user_factors
    residual = target - operator_apply(solution, gram, item_rows, extra_weight)
    direction = residual
    squares = jnp.sum(residual * residual, axis=1)
    collected = [jnp.sum(squares)]
    for _ in range(ITERS):
        image = operator_apply(direction, gram, item_rows, extra_weight)
        alpha = squares / (jnp.sum(direction * image, axis=1) + tiny)
        solution = solution + alpha[:, None] * direction
        residual = residual - alpha[:, None] * image
        fresh = jnp.sum(residual * residual, axis=1)
        direction = residual + (fresh / (squares + tiny))[:, None] * direction
        squares = fresh
        collected.append(jnp.sum(squares))
    totals = jnp.stack([global_squares(value) for value in collected])
    users_total = user_count * lax.axis_size(BLK) * lax.axis_size("rep")
    return (solution, jnp.sqrt(totals / (users_total * width)))


def solution(mesh):
    split = Mesh(
        mesh.devices.reshape(4, 8, 4, mesh.shape["rep"]), ("blk_0", "blk_1", "blk_2", "rep")
    )
    in_specs = (P(BLK, None), P(BLK_REP, None), P(BLK_REP, None), P(BLK_REP), P(BLK_REP, None))
    out_specs = (P(BLK_REP, None), P())
    return jax.shard_map(body, mesh=split, in_specs=in_specs, out_specs=out_specs, check_vma=False)
```

profile of v0, /device:TPU:1, one launch (start us, length us, event | category | flops | bytes accessed | tf_op | source)
XLA Modules:
  0.0 366.3 jit_solution(18274535382460058586)
XLA Ops:
  7.2 0.8 add_select_fusion
  8.0 4.4 %sort.17 = (s32[1024]{0:T(1024)}, s32[1024]{0:T(1024)S(1)}) sort(s32[1024]{0:T(1024)S(1)} %get-tuple-element.128, s32[1024]{0:T(1024)S(1)} %iota.14), dimensions={0}, to_apply=%region_0.0 | sort | flops 10240 | bytes 16384 | tf_op jit(solution)/shard_map/jit(argsort)/sort | solution.py:72
  12.4 4.5 %gather_fusion.1 = s32[1024]{0:T(1024)S(1)} fusion(s32[1024]{0:T(1024)S(1)} %get-tuple-element.128, s32[1024]{0:T(1024)S(1)} %get-tuple-element.129), kind=kCustom, calls=%fused_computation.1 | custom fusion | bytes 12288 | tf_op jit(solution)/shard_map/gather | solution.py:73
  16.9 13.7 %while.24 = (s32[]{:T(128)}, u32[129]{0:T(256)S(1)}, u32[129]{0:T(256)S(1)}, s32[1024]{0:T(1024)S(1)}, s32[]{:T(128)}, /*index=5*/s32[]{:T(128)}, s32[]{}) while((s32[]{:T(128)}, u32[129]{0:T(256)S(1)}, u32[129]{0:T(256)S(1)}, s32[1024]{0:T(1024)S(1)}, s32[]{:T(128)}, /*index=5*/s32[]{:T(128)}, s32[]{}) %tuple.51), condition=%wide.region_2.0_spmd.clone, body=%wide.region_1.0_spmd.clone.sunk | while | flops 2705 | bytes 10388 | solution.py:74
  17.0 1.2 gather_fusion
  18.2 1.2 gather_fusion
  19.4 1.2 gather_fusion
  20.7 1.2 gather_fusion
  21.9 1.2 gather_fusion
  23.2 1.2 gather_fusion
  24.4 1.2 gather_fusion
  25.6 1.2 gather_fusion
  26.9 1.2 gather_fusion
  28.1 1.2 gather_fusion
  29.4 1.2 gather_fusion
  30.6 6.8 %gather_fusion.2 = s32[1024]{0:T(1024)S(1)} fusion(s32[129]{0:T(256)S(1)} %convert_element_type.14, s32[1024]{0:T(1024)S(1)} %broadcast_clamp_fusion), kind=kCustom, calls=%fused_computation.2 | custom fusion | bytes 12288 | tf_op jit(solution)/shard_map/gather | solution.py:75
  37.4 4.3 %scatter_custom_fusion = s32[1024]{0:T(1024)S(1)} fusion(s32[1024]{0:T(1024)S(1)} %get-tuple-element.130, s32[1024]{0:T(1024)S(1)} %add_select_fusion.2, s32[]{:T(128)} %constant.80.clone.1), kind=kCustom, calls=%fused_computation.76 | custom fusion | bytes 4100 | tf_op jit(solution)/shard_map/scatter | solution.py:79
  41.8 4.3 %scatter_custom_fusion.1 = s32[1537]{0:T(1024)S(1)} fusion(s32[1024]{0:T(1024)S(1)} %get-tuple-element.126, s32[1024]{0:T(1024)S(1)} %get-tuple-element.127, s32[]{:T(128)} %constant.80.clone.1), kind=kCustom, calls=%fused_computation.66 | custom fusion | bytes 6152 | tf_op jit(solution)/shard_map/scatter | solution.py:80
  46.1 0.1 reshape_reshape_reshape.3
  46.2 0.1 reshape.175
  46.4 8.8 %all_to_all.20 = s32[4,1,384]{2,1,0:T(1,128)S(1)} all-to-all(s32[4,1,384]{2,1,0:T(1,128)S(1)} %reshape.175), channel_id=1, replica_groups=mesh['blk_0'=4,'blk_1'=8,'blk_2'=4,'rep'=2] {'blk_0'}, dimensions={0} | all-to-all | bytes 12288 | tf_op jit(solution)/shard_map/all_to_all | solution.py:39
  55.2 0.5 broadcast.159
  55.7 0.7 reduce.4
  56.3 0.1 reshape.176
  56.5 0.1 reshape.177
  56.6 14.6 %all_to_all.21 = s32[8,1,192]{2,1,0:T(1,128)S(1)} all-to-all(s32[8,1,192]{2,1,0:T(1,128)S(1)} %reshape.177), channel_id=1, replica_groups=mesh['blk_0'=4,'blk_1'=8,'blk_2'=4,'rep'=2] {'blk_1'}, dimensions={0} | all-to-all | bytes 12288 | tf_op jit(solution)/shard_map/all_to_all | solution.py:39
  71.2 0.7 reduce.5
  71.9 0.1 reshape.178
  72.1 8.1 %all_to_all.22 = s32[4,1,384]{2,1,0:T(1,128)S(1)} all-to-all(s32[4,1,384]{2,1,0:T(1,128)S(1)} %reshape.179), channel_id=1, replica_groups=mesh['blk_0'=4,'blk_1'=8,'blk_2'=4,'rep'=2] {'blk_2'}, dimensions={0} | all-to-all | bytes 12288 | tf_op jit(solution)/shard_map/all_to_all | solution.py:39
  80.3 0.7 reduce.6
  81.3 4.8 %gather_fusion.3 = bf16[1536,256]{1,0:T(8,128)(2,1)S(1)} fusion(bf16[2048,256]{1,0:T(8,128)(2,1)S(1)} %copy-done, s32[2048]{0:T(1024)S(1)} %pad_clamp_fusion.1), kind=kCustom, calls=%fused_computation.3 | custom fusion | bytes 1579008 | tf_op jit(solution)/shard_map/gather | solution.py:102
  86.0 1.2 reshape.113
  87.2 6.2 %all-to-all-start.3 = ((bf16[128,12,256]{2,1,0:T(8,128)(2,1)}), bf16[128,12,256]{2,1,0:T(8,128)(2,1)S(1)}, u32[]{:S(2)}, u32[]{:S(2)}) async-start(bf16[128,12,256]{2,1,0:T(8,128)(2,1)} %reshape.113), calls=%async_computation.3 | async-start | bytes 2097152 | tf_op jit(solution)/shard_map/all_to_all | solution.py:103
  93.4 1.1 fusion.10
  94.6 52.2 %all-reduce.9.cloned.1.call-done = f32[256,256]{1,0:T(8,128)} async-done(((f32[256,256]{1,0:T(8,128)}), f32[256,256]{1,0:T(8,128)}) %all-reduce.9.cloned.1.call-update) | async-done | bytes 262160 | tf_op jit(solution)/shard_map/psum | solution.py:19
  146.9 72.6 %all-reduce.11.cloned.1.call-done = f32[256,256]{1,0:T(8,128)} async-done(((f32[256,256]{1,0:T(8,128)}), f32[256,256]{1,0:T(8,128)}) %all-reduce.11.cloned.1.call-update) | async-done | bytes 262160 | tf_op jit(solution)/shard_map/psum | solution.py:19
  219.6 50.7 %all-reduce.13.cloned.1.call-done = f32[256,256]{1,0:T(8,128)} async-done(((f32[256,256]{1,0:T(8,128)}), f32[256,256]{1,0:T(8,128)}) %all-reduce.13.cloned.1.call-update) | async-done | bytes 262160 | tf_op jit(solution)/shard_map/psum | solution.py:19
  270.3 0.2 reshape.86
  270.5 3.9 %gather_fusion.4 = bf16[1024,256]{1,0:T(8,128)(2,1)S(1)} fusion(bf16[1536,256]{1,0:T(8,128)(2,1)S(1)} %reshape.86, s32[1024]{0:T(1024)S(1)} %get-tuple-element.125), kind=kCustom, calls=%fused_computation.4 | custom fusion | bytes 1052672 | tf_op jit(solution)/shard_map/gather | solution.py:104
  274.5 0.5 fusion.18
  275.0 0.2 copy-done.3
  275.2 0.5 copy-done.4
  275.7 0.3 fusion.35
  276.1 0.3 fusion.36
  276.4 28.7 %all-reduce.15.cloned.1.call-done = f32[256,256]{1,0:T(8,128)} async-done(((f32[256,256]{1,0:T(8,128)}), f32[256,256]{1,0:T(8,128)}) %all-reduce.15.cloned.1.call-update) | async-done | bytes 262160 | tf_op jit(solution)/shard_map/psum | solution.py:19
  305.1 1.2 fusion.9
  306.3 0.5 fusion.16
  306.9 0.3 fusion.37
  307.2 0.6 copy-done.1
  307.9 0.7 multiply_reduce_fusion.8
  308.6 0.7 multiply_reduce_fusion.6
  309.4 0.5 fusion.14
  310.0 0.3 fusion.38
  310.3 0.3 multiply_reduce_fusion.2
  310.6 0.2 multiply_reduce_fusion.5
  310.9 0.5 fusion.12
  311.5 0.3 fusion.39
  311.8 0.3 multiply_reduce_fusion.1
  312.2 1.3 multiply_reduce_fusion.4
  313.5 8.8 %all-reduce.2 = (f32[]{:T(128)}, f32[]{:T(128)}, f32[]{:T(128)}, f32[]{:T(128)}) all-reduce(f32[]{:T(128)} %get-tuple-element.93, f32[]{:T(128)} %get-tuple-element.92, f32[]{:T(128)} %get-tuple-element.90, f32[]{:T(128)} %get-tuple-element.87), channel_id=1, replica_groups=mesh['blk_0'=4,'blk_1'=8,'blk_2'=4,'rep'=2] {'blk_0'}, use_global_device_ids=true, to_apply=%region_31.32 | all-reduce | flops 4 | bytes 32 | tf_op jit(solution)/shard_map/psum | solution.py:19
  322.3 14.4 %all-reduce = (f32[]{:T(128)}, f32[]{:T(128)}, f32[]{:T(128)}, f32[]{:T(128)}) all-reduce(f32[]{:T(128)} %get-tuple-element.110, f32[]{:T(128)} %get-tuple-element.111, f32[]{:T(128)} %get-tuple-element.112, f32[]{:T(128)} %get-tuple-element.113), channel_id=1, replica_groups=mesh['blk_0'=4,'blk_1'=8,'blk_2'=4,'rep'=2] {'blk_1'}, use_global_device_ids=true, to_apply=%region_32.33 | all-reduce | flops 4 | bytes 32 | tf_op jit(solution)/shard_map/psum | solution.py:19
  336.7 9.1 %all-reduce.1 = (f32[]{:T(128)}, f32[]{:T(128)}, f32[]{:T(128)}, f32[]{:T(128)}) all-reduce(f32[]{:T(128)} %get-tuple-element.102, f32[]{:T(128)} %get-tuple-element.103, f32[]{:T(128)} %get-tuple-element.104, f32[]{:T(128)} %get-tuple-element.105), channel_id=1, replica_groups=mesh['blk_0'=4,'blk_1'=8,'blk_2'=4,'rep'=2] {'blk_2'}, use_global_device_ids=true, to_apply=%region_33.34 | all-reduce | flops 4 | bytes 32 | tf_op jit(solution)/shard_map/psum | solution.py:19
  345.9 10.9 %all-reduce.3 = (f32[1]{0:T(128)}, f32[1]{0:T(128)}, f32[1]{0:T(128)}, f32[1]{0:T(128)}) all-reduce(f32[1]{0:T(128)} %bitcast.36, f32[1]{0:T(128)} %bitcast.35, f32[1]{0:T(128)} %bitcast.34, f32[1]{0:T(128)} %bitcast.33), channel_id=1, replica_groups=mesh['blk_0'=4,'blk_1'=8,'blk_2'=4,'rep'=2] {'rep'}, use_global_device_ids=true, to_apply=%region_34.35 | all-reduce | flops 4 | bytes 32 | tf_op jit(solution)/shard_map/psum | solution.py:19
  356.7 3.0 fusion.29
  (77 shorter events, 1.5 us)
Async XLA Ops:
  7.2 74.1 %copy-start = (bf16[2048,256]{1,0:T(8,128)(2,1)S(1)}, bf16[2048,256]{1,0:T(8,128)(2,1)}, u32[]{:S(2)}) copy-start(bf16[2048,256]{1,0:T(8,128)(2,1)} %param.7) | copy-start | bytes 3145732
  87.2 183.1 %all-to-all-start.3 = ((bf16[128,12,256]{2,1,0:T(8,128)(2,1)}), bf16[128,12,256]{2,1,0:T(8,128)(2,1)S(1)}, u32[]{:S(2)}, u32[]{:S(2)}) async-start(bf16[128,12,256]{2,1,0:T(8,128)(2,1)} %reshape.113), calls=%async_computation.3 | async-start | bytes 2097152 | tf_op jit(solution)/shard_map/all_to_all | solution.py:103
  93.4 53.4 %all-reduce.9.cloned.1.call-start = ((), (), s32[]{:S(2)}) async-start(), calls=%async_computation.4 | async-start | bytes 524288 | tf_op jit(solution)/shard_map/psum | solution.py:19
  94.5 125.0 %all-reduce.11.cloned.1.call-start = ((), (), s32[]{:S(2)}) async-start(), calls=%async_computation.5 | async-start | bytes 524288 | tf_op jit(solution)/shard_map/psum | solution.py:19
  146.8 123.5 %all-reduce.13.cloned.1.call-start = ((), (), s32[]{:S(2)}) async-start(), calls=%async_computation.6 | async-start | bytes 524288 | tf_op jit(solution)/shard_map/psum | solution.py:19
  219.5 85.6 %all-reduce.15.cloned.1.call-start = ((), (), s32[]{:S(2)}) async-start(), calls=%async_computation.7 | async-start | bytes 524288 | tf_op jit(solution)/shard_map/psum | solution.py:19
  270.5 4.0 %copy-start.2 = (f32[8,256]{1,0:T(8,128)S(1)}, f32[8,256]{1,0:T(8,128)}, u32[]{:S(2)}) copy-start(f32[8,256]{1,0:T(8,128)} %param.8) | copy-start | bytes 24580
  274.5 0.7 copy-start.3
  275.0 0.7 copy-start.4
  306.9 1.0 copy-start.1
Sparse Core Ops, SparseCore 0:
  96.5 50.2 all-reduce.8
  149.1 70.3 all-reduce.10
  221.9 48.3 all-reduce.12
  272.7 32.3 all-reduce.14
where the time goes:
time: 367 us; the launch traced here: 366 us
  waiting for transfers between devices  204 us (56%)
  blocking collectives  74.7 us (20%)
  local copies, waits for them, and re-layouts  45.8 us (12%)
  between operations  14.1 us (4%)
  other arithmetic  13.2 us (4%)
  matrix products  7.29 us (2%)
  starting transfers between devices  6.35 us (2%)
    psum x4, waiting for transfers between devices, over_axes(): array = lax.psum(array, axis)  204 us
    psum x4, blocking collectives, over_axes(): array = lax.psum(array, axis)  43.2 us
    all_to_all x3, blocking collectives, moved_by_axis(): lax.all_to_all(pieces, axes[k], split_axis=k, concat_axis=k, tiled=True)  31.5 us
    gather x11, local copies, waits for them, and re-layouts, pack_requests(): jnp.searchsorted(sorted_owner, jnp.arange(blocks + 1, dtype=jnp.int32))  12.9 us
  transfers between devices with their start and end apart: 5, of which 4 were waited for; matrix products, arithmetic and copies ran while one was open for 2% of the time, Pallas kernels for 0%

commit v1 on v0

v1 whole, which is shorter than its diff:
```python
import jax
import jax.numpy as jnp
from jax import lax
from jax.experimental import pallas as pl
from jax.experimental.pallas import tpu as pltpu
from jax.sharding import Mesh
from jax.sharding import PartitionSpec as P

ITERS = 3
BLK_REP = ("blk_0", "blk_1", "blk_2", "rep")
BLK = ("blk_0", "blk_1", "blk_2")
MESH = pl.DeviceIdType.MESH

NX, NZ, NY, NR = 4, 8, 4, 2
NP = NX * NY
NH = NP * NZ
CAP = 8
U, L, K = 8, 128, 256
ROWS = 2048
USERS = U * NH * NR
F32, BF16, I32 = jnp.float32, jnp.bfloat16, jnp.int32

conf_scale = 40.0
ridge = 1.0
tiny = 1e-06


def dot(a, b):
    return jnp.dot(a, b, preferred_element_type=F32)


def dot_nt(a, b):
    return lax.dot_general(a, b, (((1,), (1,)), ((), ())), preferred_element_type=F32)


def pieces(v):
    hi = v.astype(BF16)
    rest = v - hi.astype(F32)
    mid = rest.astype(BF16)
    low = (rest - mid.astype(F32)).astype(BF16)
    return hi, mid, low


def stacked(v):
    hi, mid, low = pieces(v)
    return jnp.concatenate([hi.astype(F32), mid.astype(F32), low.astype(F32)], axis=0).astype(BF16)


def folded(v, n):
    return v[:n] + v[n : 2 * n] + v[2 * n : 3 * n]


def iota(shape, dim):
    return lax.broadcasted_iota(I32, shape, dim)


def kernel(
    counts_ref,
    lists_ref,
    plays_ref,
    users_ref,
    items_hbm,
    out_ref,
    norms_ref,
    items,
    req_send,
    req_z,
    req_fwd,
    req_p,
    req_t,
    gram_mine,
    gram_p,
    gram_zsend,
    gram_z,
    gram_red,
    gram_full,
    gram3,
    rows_send,
    rows_in,
    rows_mat,
    norm_send,
    norm_p,
    norm_mid,
    norm_z,
    local_sem,
    req_sems,
    gram_sems,
    rows_sem,
    rows_recv,
    norm_sems,
):
    x, z, y, r = (lax.axis_index(a) for a in BLK_REP)
    p = x * NY + y

    def device(pp, zz, rr):
        return (pp // NY, zz, pp % NY, rr)

    def send(src, dst, send_sem, recv_sem, dev):
        pltpu.make_async_remote_copy(
            src_ref=src, dst_ref=dst, send_sem=send_sem, recv_sem=recv_sem, device_id=dev, device_id_type=MESH
        ).start()

    def wait_bytes(ref, sem):
        pltpu.make_async_copy(ref, ref, sem).wait()

    def plane_peer(k):
        both = (p * NR + r + k) % (NP * NR)
        return both // NR, both % NR

    barrier = pltpu.get_barrier_semaphore()

    @pl.loop(1, NP * NR)
    def _(k):
        pp, rr = plane_peer(k)
        pl.semaphore_signal(barrier, inc=1, device_id=device(pp, z, rr), device_id_type=MESH)

    @pl.loop(1, NZ)
    def _(k):
        pl.semaphore_signal(barrier, inc=1, device_id=device(p, (z + k) % NZ, r), device_id_type=MESH)

    items_copy = pltpu.make_async_copy(items_hbm, items, local_sem)
    items_copy.start()

    lists = lists_ref[...]
    user = iota((U, L), 0)
    count = jnp.zeros((U, L), I32)
    for u in range(U):
        count = jnp.where(user == u, counts_ref[u], count)
    live = iota((U, L), 1) < count
    block = lists >> 11
    holder = ((block >> 2) & 7) * NP + (block >> 5) * NY + (block & 3)
    local = lists & (ROWS - 1)
    holder = jnp.where(live, holder, -1)
    before = jnp.where((iota((L, 2 * L), 0) < iota((L, 2 * L), 1)) | (iota((L, 2 * L), 1) >= L), 1.0, 0.0).astype(BF16)
    base = jnp.zeros((NH, L), F32)
    ranks = []
    for u in range(U):
        hit = jnp.where(iota((NH, L), 0) == holder[u : u + 1, :], 1.0, 0.0)
        sums = dot(hit.astype(BF16), before)
        ranks.append(jnp.sum(hit * (sums[:, :L] + base), axis=0, keepdims=True))
        base = base + sums[:, L:]
    rank = jnp.concatenate(ranks, axis=0)
    place = jnp.where(live, holder.astype(F32) * CAP + rank, -1.0)
    place_t = jnp.concatenate([place, jnp.zeros((L - U, L), F32)], axis=0).T

    confidence = 1.0 + conf_scale * jnp.log(2.0 + plays_ref[...].astype(F32))
    full_weight = jnp.where(live, confidence, 0.0)
    full3 = [v.astype(F32) for v in pieces(full_weight)]
    id_hi = (local >> 4).astype(F32)
    id_lo = (local & 15).astype(F32)
    found = jnp.zeros((4 * U, NH * CAP), F32)
    for u in range(U):
        pick = jnp.where(place_t[:, u : u + 1] == iota((L, NH * CAP), 1).astype(F32), 1.0, 0.0).astype(BF16)
        names = jnp.where(user == 0, id_hi[u : u + 1, :], jnp.where(user == 1, id_lo[u : u + 1, :], 0.0))
        left = jnp.concatenate([jnp.where(user == u, v, 0.0) for v in full3] + [names], axis=0).astype(BF16)
        found = found + dot(left, pick)
    weight = folded(found, U)
    extra = jnp.where(weight > 0.0, weight - 1.0, 0.0)
    wanted = found[3 * U : 3 * U + 1] * 16.0 + found[3 * U + 1 : 3 * U + 2]
    for k in range(NZ):
        req_send[k] = wanted[:, k * L : (k + 1) * L]
    req_z[z] = req_send[z]

    pl.semaphore_wait(barrier, NP * NR - 1 + NZ - 1)

    @pl.loop(1, NZ)
    def _(k):
        zz = (z + k) % NZ
        send(req_send.at[zz], req_z.at[z], req_sems.at[0], req_sems.at[1], device(p, zz, r))

    items_copy.wait()
    half = pl.ds(pl.multiple_of(r * (K // NR), K // NR), K // NR)
    part = lax.dot_general(items[:, half], items[...], (((0,), (0,)), ((), ())), preferred_element_type=F32)
    gram_mine[...] = part.reshape(NP, 8, K)
    gram_p[p] = gram_mine[p]

    @pl.loop(1, NP)
    def _(k):
        pp = (p + k) % NP
        send(gram_mine.at[pp], gram_p.at[p], gram_sems.at[0], gram_sems.at[1], device(pp, z, r))

    wait_bytes(req_send.at[pl.ds(0, NZ - 1)], req_sems.at[0])
    wait_bytes(req_z.at[pl.ds(0, NZ - 1)], req_sems.at[1])
    req_fwd[...] = req_z[...].reshape(NZ, L)
    req_p[p] = req_fwd[...]

    @pl.loop(1, NP)
    def _(k):
        send(req_fwd, req_p.at[p], req_sems.at[2], req_sems.at[3], device((p + k) % NP, z, r))

    wait_bytes(gram_mine.at[pl.ds(0, NP - 1)], gram_sems.at[0])
    wait_bytes(gram_p.at[pl.ds(0, NP - 1)], gram_sems.at[1])
    gram_zsend[...] = jnp.sum(gram_p[...], axis=0)
    gram_z[z] = gram_zsend[...]

    @pl.loop(1, NZ)
    def _(k):
        send(gram_zsend, gram_z.at[z], gram_sems.at[2], gram_sems.at[3], device(p, (z + k) % NZ, r))

    wait_bytes(req_p.at[pl.ds(0, NP - 1)], req_sems.at[2])
    wait_bytes(req_p.at[pl.ds(0, NP - 1)], req_sems.at[3])
    req_t[...] = req_p[...].reshape(NP * NZ, L).T
    asked = req_t[pl.ds(pl.multiple_of(p * CAP, CAP), CAP), :]
    first = 3
    asked = pltpu.roll(asked, (L - z - first) % L, axis=1)

    def serve(step, asked):
        column = jnp.concatenate([asked[:, i * NZ : i * NZ + 1] for i in range(NP)], axis=0)
        total = jnp.zeros((NP * CAP, K), F32)
        width = 512
        for part in range(ROWS // width):
            pick = jnp.where(column == (iota((NP * CAP, width), 1) + part * width).astype(F32), 1.0, 0.0).astype(BF16)
            total = total + dot(pick, items[part * width : (part + 1) * width, :])
        rows_send[pl.ds(pl.multiple_of(step * NP, NP), NP)] = total.reshape(NP, CAP, K).astype(BF16)

        @pl.loop(0, NP)
        def _(i):
            to = (i * NZ + step + z + first) % (NP * NZ)
            pp, zz = to // NZ, to % NZ
            mine = to == p * NZ + z
            src = rows_send.at[step * NP + i]
            dst = rows_in.at[z * NP + p]

            @pl.when(mine)
            def _():
                pltpu.make_async_copy(src, dst, rows_recv.at[z]).start()

            @pl.when(jnp.logical_not(mine))
            def _():
                send(src, dst, rows_sem, rows_recv.at[z], device(pp, zz, r))

        return pltpu.roll(asked, L - 1, axis=1)

    lax.fori_loop(0, NZ, serve, asked)

    wait_bytes(gram_z.at[pl.ds(0, NZ - 1)], gram_sems.at[2])
    wait_bytes(gram_z.at[pl.ds(0, NZ - 1)], gram_sems.at[3])
    gram_red[...] = jnp.sum(gram_z[...], axis=0)
    gram_full[r * NP + p] = gram_red[...]

    @pl.loop(1, NP * NR)
    def _(k):
        pp, rr = plane_peer(k)
        send(gram_red, gram_full.at[r * NP + p], gram_sems.at[4], gram_sems.at[5], device(pp, z, rr))

    wait_bytes(gram_full.at[pl.ds(0, NP * NR - 1)], gram_sems.at[4])
    wait_bytes(gram_full.at[pl.ds(0, NP * NR - 1)], gram_sems.at[5])
    for k, piece in enumerate(pieces(gram_full[...].reshape(K, K))):
        gram3[:, k * K : (k + 1) * K] = piece

    for k in range(NZ):
        wait_bytes(rows_in.at[pl.ds(k * NP, NP)], rows_recv.at[k])
        rows_mat[k * L : (k + 1) * L, :] = rows_in[k * NP : (k + 1) * NP].astype(F32).reshape(L, K).astype(BF16)
    wait_bytes(rows_send.at[pl.ds(0, NH - 1)], rows_sem)

    def image_of(v):
        v3 = stacked(v)
        along = folded(dot_nt(v3, rows_mat[...]), U)
        back = folded(dot(stacked(extra * along), rows_mat[...]), U)
        g = folded(dot(v3, gram3[...]), U)
        return g[:, :K] + g[:, K : 2 * K] + g[:, 2 * K :] + back + ridge * v

    def inner(a, b):
        return jnp.sum(a * b, axis=1, keepdims=True)

    target = folded(dot(stacked(weight), rows_mat[...]), U)
    solution = users_ref[...]
    residual = target - image_of(solution)
    direction = residual
    squares = inner(residual, residual)
    lane = iota((U, L), 1)
    collected = jnp.where(lane == 0, squares, 0.0)
    for t in range(ITERS):
        image = image_of(direction)
        alpha = squares / (inner(direction, image) + tiny)
        solution = solution + alpha * direction
        residual = residual - alpha * image
        fresh = inner(residual, residual)
        direction = residual + (fresh / (squares + tiny)) * direction
        squares = fresh
        collected = collected + jnp.where(lane == t + 1, squares, 0.0)
    out_ref[...] = solution

    norm_send[...] = jnp.sum(collected, axis=0, keepdims=True)
    norm_p[p * NR + r] = norm_send[...]

    @pl.loop(1, NP * NR)
    def _(k):
        pp, rr = plane_peer(k)
        send(norm_send, norm_p.at[p * NR + r], norm_sems.at[0], norm_sems.at[1], device(pp, z, rr))

    wait_bytes(norm_p.at[pl.ds(0, NP * NR - 1)], norm_sems.at[0])
    wait_bytes(norm_p.at[pl.ds(0, NP * NR - 1)], norm_sems.at[1])
    norm_mid[...] = jnp.sum(norm_p[...], axis=0)
    norm_z[z] = norm_mid[...]

    @pl.loop(1, NZ)
    def _(k):
        send(norm_mid, norm_z.at[z], norm_sems.at[2], norm_sems.at[3], device(p, (z + k) % NZ, r))

    wait_bytes(norm_z.at[pl.ds(0, NZ - 1)], norm_sems.at[2])
    wait_bytes(norm_z.at[pl.ds(0, NZ - 1)], norm_sems.at[3])
    total = jnp.sum(norm_z[...], axis=0)
    norms_ref[...] = jnp.sqrt(total / (USERS * K))[:, : ITERS + 1]


def body(item_factors, user_factors, item_lists, counts, plays):
    vmem = pl.BlockSpec(memory_space=pltpu.VMEM)
    dma = pltpu.SemaphoreType.DMA
    new_factors, norms = pl.pallas_call(
        kernel,
        out_shape=(jax.ShapeDtypeStruct((U, K), F32), jax.ShapeDtypeStruct((1, ITERS + 1), F32)),
        in_specs=[pl.BlockSpec(memory_space=pltpu.SMEM), vmem, vmem, vmem, pl.BlockSpec(memory_space=pl.ANY)],
        out_specs=(vmem, vmem),
        scratch_shapes=[
            pltpu.VMEM((ROWS, K), BF16),
            pltpu.VMEM((NZ, 1, L), F32),
            pltpu.VMEM((NZ, 1, L), F32),
            pltpu.VMEM((NZ, L), F32),
            pltpu.VMEM((NP, NZ, L), F32),
            pltpu.VMEM((L, NP * NZ), F32),
            pltpu.VMEM((NP, 8, K), F32),
            pltpu.VMEM((NP, 8, K), F32),
            pltpu.VMEM((8, K), F32),
            pltpu.VMEM((NZ, 8, K), F32),
            pltpu.VMEM((8, K), F32),
            pltpu.VMEM((NR * NP, 8, K), F32),
            pltpu.VMEM((K, 3 * K), BF16),
            pltpu.VMEM((NH, CAP, K), BF16),
            pltpu.VMEM((NH, CAP, K), BF16),
            pltpu.VMEM((NH * CAP, K), BF16),
            pltpu.VMEM((1, L), F32),
            pltpu.VMEM((NP * NR, 1, L), F32),
            pltpu.VMEM((1, L), F32),
            pltpu.VMEM((NZ, 1, L), F32),
            dma,
            dma((4,)),
            dma((6,)),
            dma,
            dma((NZ,)),
            dma((4,)),
        ],
        compiler_params=pltpu.CompilerParams(collective_id=0, has_side_effects=True),
    )(counts, item_lists, plays, user_factors, item_factors)
    return new_factors, norms.reshape(ITERS + 1)


def solution(mesh):
    split = Mesh(mesh.devices.reshape(NX, NZ, NY, NR), BLK_REP)
    in_specs = (P(BLK, None), P(BLK_REP, None), P(BLK_REP, None), P(BLK_REP), P(BLK_REP, None))
    out_specs = (P(BLK_REP, None), P())
    return jax.shard_map(body, mesh=split, in_specs=in_specs, out_specs=out_specs, check_vma=False)
```

time: 367 us -> 52 us (0.14)
  waiting for transfers between devices: 204 us -> 0 us
  blocking collectives: 74.7 us -> 0 us
  Pallas kernels: 0 us -> 49.4 us
  local copies, waits for them, and re-layouts: 45.8 us -> 1.81 us
  between operations: 14.1 us -> 0.65 us
  other arithmetic: 13.2 us -> 0 us
  matrix products: 7.29 us -> 0 us
  starting transfers between devices: 6.35 us -> 0 us
    psum x4 -> x0, waiting for transfers between devices: 204 us -> none  [over_axes(): array = lax.psum(array, axis)]
    pallas_call x0 -> x1, Pallas kernels: none -> 49.4 us  [body(): pl.pallas_call(kernel, out_shape=(jax.ShapeDtypeStruct((U, K), F32), jax....]
    psum x4 -> x0, blocking collectives: 43.2 us -> none  [over_axes(): array = lax.psum(array, axis)]
    gather x16 -> x0, local copies, waits for them, and re-layouts: 34.1 us -> none  [the longest x11 12.9 us: pack_requests(): jnp.searchsorted(sorted_owner, jnp.arange(blocks + 1, dtype=jnp.int32))]
    all_to_all x3 -> x0, blocking collectives: 31.5 us -> none  [moved_by_axis(): lax.all_to_all(pieces, axes[k], split_axis=k, concat_axis=k, tiled=True)]
    scatter x2 -> x0, local copies, waits for them, and re-layouts: 8.63 us -> none  [the longest x1 4.32 us: pack_requests(): jnp.zeros((blocks * capacity + 1,), jnp.int32).at[place].set(local)]
    dot_general x14 -> x0, matrix products: 7.29 us -> none  [the longest x4 2.55 us: operator_apply(): jnp.dot(vector, gram, precision=lax.Precision.HIGHEST) + back]
    all_to_all x1 -> x0, starting transfers between devices: 6.19 us -> none  [body(): reply = lax.all_to_all(found, BLK, split_axis=0, concat_axis=0, tiled=True)]
  transfers between devices with their start and end apart: 5 -> 0, of which waited for: 4 -> 0; matrix products, arithmetic and copies ran while one was open for 2% -> 0% of each run, Pallas kernels for 0% -> 0%
where the time goes in v1:
time: 52 us; the launch traced here: 51.8 us
  Pallas kernels  49.4 us (95%)
  local copies, waits for them, and re-layouts  1.81 us (3%)
  between operations  0.65 us (1%)
    pallas_call x1, Pallas kernels, body(): pl.pallas_call(kernel, out_shape=(jax.ShapeDtypeStruct((U, K), F32), jax....  49.4 us
    unnamed x4, local copies, waits for them, and re-layouts  1.81 us

profile of v1, /device:TPU:1, one launch (start us, length us, event | category | flops | bytes accessed | tf_op | source)
XLA Modules:
  0.0 51.8 jit_solution(17229248284162031552)
XLA Ops:
  0.6 49.4 %shard_map.68 = (f32[8,256]{1,0:T(8,128)}, f32[1,4]{1,0:T(1,128)}) custom-call(s32[8]{0:T(128)} %counts_ref.1, s32[8,128]{1,0:T(8,128)} %lists_ref.1, s32[8,128]{1,0:T(8,128)} %plays_ref.1, f32[8,256]{1,0:T(8,128)} %users_ref.1, bf16[2048,256]{1,0:T(8,128)(2,1)} %items_hbm.1), custom_call_target="tpu_custom_call" | custom-call | tf_op jit(solution)/shard_map/pallas_call | solution.py:310
  50.0 0.0 copy-start
  50.0 1.3 %copy.9 = f32[8,256]{1,0:T(8,128)} copy(f32[8,256]{1,0:T(8,128)} %get-tuple-element.8) | data formatting | bytes 16384
  51.3 0.0 copy-done
  51.3 0.5 copy.10
Async XLA Ops:
  50.0 1.3 %copy-start = (f32[1,4]{1,0:T(1,128)S(1)}, f32[1,4]{1,0:T(1,128)}, u32[]{:S(2)}) copy-start(f32[1,4]{1,0:T(1,128)} %get-tuple-element.5) | copy-start | bytes 52

commit v2 on v1

v2 whole, which is shorter than its diff:
```python
import jax
import jax.numpy as jnp
from jax import lax
from jax.experimental import pallas as pl
from jax.experimental.pallas import tpu as pltpu
from jax.sharding import Mesh
from jax.sharding import PartitionSpec as P

ITERS = 3
BLK_REP = ("blk_0", "blk_1", "blk_2", "rep")
BLK = ("blk_0", "blk_1", "blk_2")
MESH = pl.DeviceIdType.MESH

NX, NZ, NY, NR = 4, 8, 4, 2
NP = NX * NY
NH = NP * NZ
CAP = 8
U, L, K = 8, 128, 256
ROWS = 2048
USERS = U * NH * NR
GRAM_AFTER = 2
F32, BF16, I32 = jnp.float32, jnp.bfloat16, jnp.int32

conf_scale = 40.0
ridge = 1.0
tiny = 1e-06


def dot(a, b):
    return jnp.dot(a, b, preferred_element_type=F32)


def dot_nt(a, b):
    return lax.dot_general(a, b, (((1,), (1,)), ((), ())), preferred_element_type=F32)


def pieces(v):
    hi = v.astype(BF16)
    rest = v - hi.astype(F32)
    mid = rest.astype(BF16)
    low = (rest - mid.astype(F32)).astype(BF16)
    return hi, mid, low


def stacked(v):
    hi, mid, low = pieces(v)
    return jnp.concatenate([hi.astype(F32), mid.astype(F32), low.astype(F32)], axis=0).astype(BF16)


def folded(v, n):
    return v[:n] + v[n : 2 * n] + v[2 * n : 3 * n]


def iota(shape, dim):
    return lax.broadcasted_iota(I32, shape, dim)


class Phases:
    def __init__(self):
        self.open = None

    def __call__(self, name):
        if self.open is not None:
            self.open.__exit__(None, None, None)
        self.open = jax.named_scope(name) if name else None
        if self.open is not None:
            self.open.__enter__()


NEAR = sorted(((dx, dy) for dx in range(NX) for dy in range(NY)), key=lambda d: (min(d[0], NX - d[0]) + min(d[1], NY - d[1]), d))
FAR_Z = (4, 3, 5, 2, 6, 1, 7, 0)


def kernel(
    counts_hbm,
    lists_hbm,
    plays_hbm,
    users_hbm,
    items_hbm,
    out_ref,
    norms_ref,
    counts_ref,
    lists_ref,
    plays_ref,
    users_ref,
    items,
    req_send,
    req_z,
    req_fwd,
    req_p,
    gram_mine,
    gram_p,
    gram_zsend,
    gram_z,
    gram_red,
    gram_full,
    gram3,
    rows_send,
    rows_in,
    rows_mat,
    norm_send,
    norm_p,
    norm_mid,
    norm_z,
    local_sems,
    req_sems,
    req_recv,
    gram_sems,
    rows_sem,
    rows_recv,
    norm_sems,
):
    phase = Phases()
    phase("enter")
    x, z, y, r = (lax.axis_index(a) for a in BLK_REP)
    p = x * NY + y

    def plane_device(d, same=1):
        return ((x + d[0]) & (NX - 1), z, (y + d[1]) & (NY - 1), r if same else 1 - r)

    def z_device(dz):
        return (x, (z + dz) & (NZ - 1), y, r)

    def place_of(dev):
        return dev[0] * NY + dev[2]

    peers = [(d, same) for same in (1, 0) for d in reversed(NEAR) if not (same and d == (0, 0))]

    def send(src, dst, send_sem, recv_sem, dev):
        pltpu.make_async_remote_copy(
            src_ref=src, dst_ref=dst, send_sem=send_sem, recv_sem=recv_sem, device_id=dev, device_id_type=MESH
        ).start()

    def wait_bytes(ref, sem):
        pltpu.make_async_copy(ref, ref, sem).wait()

    copies = [
        pltpu.make_async_copy(src, dst, local_sems.at[k])
        for k, (src, dst) in enumerate(
            [(counts_hbm, counts_ref), (lists_hbm, lists_ref), (plays_hbm, plays_ref), (users_hbm, users_ref), (items_hbm, items)]
        )
    ]
    for copy in copies:
        copy.start()
    barrier = pltpu.get_barrier_semaphore()
    for dz in range(1, NZ):
        pl.semaphore_signal(barrier, inc=1, device_id=z_device(dz), device_id_type=MESH)
    for d, same in peers:
        pl.semaphore_signal(barrier, inc=1, device_id=plane_device(d, same), device_id_type=MESH)
    for copy in copies[:3]:
        copy.wait()

    phase("pack")
    lists = lists_ref[...]
    user = iota((U, L), 0)
    count = jnp.zeros((U, L), I32)
    for u in range(U):
        count = jnp.where(user == u, counts_ref[u], count)
    live = iota((U, L), 1) < count
    block = lists >> 11
    holder = ((block >> 2) & 7) * NP + (block >> 5) * NY + (block & 3)
    local = lists & (ROWS - 1)
    holder = jnp.where(live, holder, -1)
    before = jnp.where((iota((L, 2 * L), 0) < iota((L, 2 * L), 1)) | (iota((L, 2 * L), 1) >= L), 1.0, 0.0).astype(BF16)
    base = jnp.zeros((NH, L), F32)
    ranks = []
    for u in range(U):
        hit = jnp.where(iota((NH, L), 0) == holder[u : u + 1, :], 1.0, 0.0)
        sums = dot(hit.astype(BF16), before)
        ranks.append(jnp.sum(hit * (sums[:, :L] + base), axis=0, keepdims=True))
        base = base + sums[:, L:]
    rank = jnp.concatenate(ranks, axis=0)
    place = jnp.where(live, holder.astype(F32) * CAP + rank, -1.0)
    place_t = jnp.concatenate([place, jnp.zeros((L - U, L), F32)], axis=0).T

    phase("weights")
    confidence = 1.0 + conf_scale * jnp.log(2.0 + plays_ref[...].astype(F32))
    full_weight = jnp.where(live, confidence, 0.0)
    full3 = [v.astype(F32) for v in pieces(full_weight)]
    id_hi = (local >> 4).astype(F32)
    id_lo = (local & 15).astype(F32)
    found = jnp.zeros((4 * U, NH * CAP), F32)
    for u in range(U):
        pick = jnp.where(place_t[:, u : u + 1] == iota((L, NH * CAP), 1).astype(F32), 1.0, 0.0).astype(BF16)
        names = jnp.where(user == 0, id_hi[u : u + 1, :], jnp.where(user == 1, id_lo[u : u + 1, :], 0.0))
        left = jnp.concatenate([jnp.where(user == u, v, 0.0) for v in full3] + [names], axis=0).astype(BF16)
        found = found + dot(left, pick)
    weight = folded(found, U)
    extra = jnp.where(weight > 0.0, weight - 1.0, 0.0)
    wanted = found[3 * U : 3 * U + 1] * 16.0 + found[3 * U + 1 : 3 * U + 2]
    for k in range(NZ):
        req_send[k] = wanted[:, k * L : (k + 1) * L]
    req_z[0] = req_send[z]

    phase("barrier")
    pl.semaphore_wait(barrier, NP * NR - 1 + NZ - 1)
    for dz in FAR_Z[:-1]:
        dev = z_device(dz)
        send(req_send.at[dev[1]], req_z.at[NZ - dz], req_sems.at[0], req_sems.at[1], dev)

    phase("gram")
    copies[4].wait()
    half = pl.ds(pl.multiple_of(r * (K // NR), K // NR), K // NR)
    part = lax.dot_general(items[:, half], items[...], (((0,), (0,)), ((), ())), preferred_element_type=F32)
    gram_mine[...] = part.reshape(NP, 8, K)
    gram_p[p] = gram_mine[p]
    phase("gram_p_send")
    for d in reversed(NEAR[1:]):
        dev = plane_device(d)
        send(gram_mine.at[place_of(dev)], gram_p.at[p], gram_sems.at[0], gram_sems.at[1], dev)

    phase("req_z_wait")
    wait_bytes(req_z.at[pl.ds(0, NZ - 1)], req_sems.at[1])
    req_fwd[...] = jnp.concatenate([req_z[...].reshape(NZ, L), jnp.zeros((L - NZ, L), F32)], axis=0).T.reshape(NP, CAP, L)
    phase("req_p_send")
    for k in reversed(range(1, NP)):
        dev = plane_device(NEAR[k])
        send(req_fwd.at[place_of(dev)], req_p.at[k], req_sems.at[2], req_recv.at[k], dev)

    phase("gram_p_wait")
    wait_bytes(gram_p.at[pl.ds(0, NP - 1)], gram_sems.at[1])
    gram_zsend[...] = jnp.sum(gram_p[...], axis=0)
    gram_z[z] = gram_zsend[...]
    for dz in FAR_Z[:-1]:
        send(gram_zsend, gram_z.at[z], gram_sems.at[2], gram_sems.at[3], z_device(dz))

    def serve(step):
        tiles = []
        for k in (2 * step, 2 * step + 1):
            if k:
                wait_bytes(req_p.at[k], req_recv.at[k])
            tiles.append(req_p[k] if k else req_fwd[p])
        column = jnp.concatenate([t[:, dz : dz + 1] for t in tiles for dz in FAR_Z], axis=0)
        total = jnp.zeros((2 * NZ * CAP, K), F32)
        width = 512
        for part in range(ROWS // width):
            pick = jnp.where(column == (iota((2 * NZ * CAP, width), 1) + part * width).astype(F32), 1.0, 0.0).astype(BF16)
            total = total + dot(pick, items[part * width : (part + 1) * width, :])
        rows_send[step] = total.reshape(2 * NZ, CAP, K).astype(BF16)
        for i in range(2):
            d = NEAR[2 * step + i]
            for j, dz in enumerate(FAR_Z):
                dev = ((x - d[0]) & (NX - 1), (z + dz) & (NZ - 1), (y - d[1]) & (NY - 1), r)
                src = rows_send.at[step, i * NZ + j]
                dst = rows_in.at[z * NP + p]
                if d == (0, 0) and dz == 0:
                    pltpu.make_async_copy(src, dst, rows_recv).start()
                else:
                    send(src, dst, rows_sem, rows_recv, dev)

    def spread_gram():
        wait_bytes(gram_z.at[pl.ds(0, NZ - 1)], gram_sems.at[3])
        gram_red[...] = jnp.sum(gram_z[...], axis=0)
        gram_full[r * NP + p] = gram_red[...]
        for d, same in peers:
            send(gram_red, gram_full.at[r * NP + p], gram_sems.at[4], gram_sems.at[5], plane_device(d, same))

    for step in range(NP // 2):
        phase("serve%d" % step)
        serve(step)
        if step == GRAM_AFTER:
            phase("gram_ag")
            spread_gram()

    phase("gram_ag_wait")
    wait_bytes(gram_full.at[pl.ds(0, NP * NR - 1)], gram_sems.at[5])
    phase("gram_pieces")
    for k, piece in enumerate(pieces(gram_full[...].reshape(K, K))):
        gram3[:, k * K : (k + 1) * K] = piece

    phase("rows_wait")
    wait_bytes(rows_in, rows_recv)
    rows_mat[...] = rows_in[...].astype(F32).reshape(NH * CAP, K).astype(BF16)

    phase("cg")
    def image_of(v):
        v3 = stacked(v)
        along = folded(dot_nt(v3, rows_mat[...]), U)
        back = folded(dot(stacked(extra * along), rows_mat[...]), U)
        g = folded(dot(v3, gram3[...]), U)
        return g[:, :K] + g[:, K : 2 * K] + g[:, 2 * K :] + back + ridge * v

    def inner(a, b):
        return jnp.sum(a * b, axis=1, keepdims=True)

    target = folded(dot(stacked(weight), rows_mat[...]), U)
    copies[3].wait()
    solution = users_ref[...]
    residual = target - image_of(solution)
    direction = residual
    squares = inner(residual, residual)
    lane = iota((U, L), 1)
    collected = jnp.where(lane == 0, squares, 0.0)
    for t in range(ITERS):
        image = image_of(direction)
        alpha = squares / (inner(direction, image) + tiny)
        solution = solution + alpha * direction
        residual = residual - alpha * image
        fresh = inner(residual, residual)
        direction = residual + (fresh / (squares + tiny)) * direction
        squares = fresh
        collected = collected + jnp.where(lane == t + 1, squares, 0.0)

    norm_send[...] = jnp.sum(collected, axis=0, keepdims=True)
    phase("norm_p")
    norm_p[p * NR + r] = norm_send[...]
    for d, same in peers:
        send(norm_send, norm_p.at[p * NR + r], norm_sems.at[0], norm_sems.at[1], plane_device(d, same))
    out_ref[...] = solution
    wait_bytes(req_z.at[pl.ds(0, NZ - 1)], req_sems.at[0])
    wait_bytes(req_p.at[pl.ds(0, NP - 1)], req_sems.at[2])
    wait_bytes(gram_mine.at[pl.ds(0, NP - 1)], gram_sems.at[0])
    wait_bytes(gram_z.at[pl.ds(0, NZ - 1)], gram_sems.at[2])
    wait_bytes(gram_full.at[pl.ds(0, NP * NR - 1)], gram_sems.at[4])
    wait_bytes(rows_in.at[pl.ds(0, NH - 1)], rows_sem)
    wait_bytes(norm_p.at[pl.ds(0, NP * NR - 1)], norm_sems.at[1])
    norm_mid[...] = jnp.sum(norm_p[...], axis=0)
    phase("norm_z")
    norm_z[z] = norm_mid[...]
    for dz in FAR_Z[:-1]:
        send(norm_mid, norm_z.at[z], norm_sems.at[2], norm_sems.at[3], z_device(dz))
    wait_bytes(norm_p.at[pl.ds(0, NP * NR - 1)], norm_sems.at[0])
    wait_bytes(norm_z.at[pl.ds(0, NZ - 1)], norm_sems.at[3])
    phase("norm_end")
    total = jnp.sum(norm_z[...], axis=0)
    norms_ref[...] = jnp.sqrt(total / (USERS * K))[:, : ITERS + 1]
    wait_bytes(norm_z.at[pl.ds(0, NZ - 1)], norm_sems.at[2])
    phase(None)


def body(item_factors, user_factors, item_lists, counts, plays):
    vmem = pl.BlockSpec(memory_space=pltpu.VMEM)
    dma = pltpu.SemaphoreType.DMA
    new_factors, norms = pl.pallas_call(
        kernel,
        out_shape=(jax.ShapeDtypeStruct((U, K), F32), jax.ShapeDtypeStruct((1, ITERS + 1), F32)),
        in_specs=[pl.BlockSpec(memory_space=pl.ANY)] * 5,
        out_specs=(vmem, vmem),
        scratch_shapes=[
            pltpu.SMEM((U,), I32),
            pltpu.VMEM((U, L), I32),
            pltpu.VMEM((U, L), I32),
            pltpu.VMEM((U, K), F32),
            pltpu.VMEM((ROWS, K), BF16),
            pltpu.VMEM((NZ, 1, L), F32),
            pltpu.VMEM((NZ, 1, L), F32),
            pltpu.VMEM((NP, CAP, L), F32),
            pltpu.VMEM((NP, CAP, L), F32),
            pltpu.VMEM((NP, 8, K), F32),
            pltpu.VMEM((NP, 8, K), F32),
            pltpu.VMEM((8, K), F32),
            pltpu.VMEM((NZ, 8, K), F32),
            pltpu.VMEM((8, K), F32),
            pltpu.VMEM((NR * NP, 8, K), F32),
            pltpu.VMEM((K, 3 * K), BF16),
            pltpu.VMEM((NP // 2, 2 * NZ, CAP, K), BF16),
            pltpu.VMEM((NH, CAP, K), BF16),
            pltpu.VMEM((NH * CAP, K), BF16),
            pltpu.VMEM((1, L), F32),
            pltpu.VMEM((NP * NR, 1, L), F32),
            pltpu.VMEM((1, L), F32),
            pltpu.VMEM((NZ, 1, L), F32),
            dma((5,)),
            dma((3,)),
            dma((NP,)),
            dma((6,)),
            dma,
            dma,
            dma((4,)),
        ],
        compiler_params=pltpu.CompilerParams(collective_id=0, has_side_effects=True),
    )(counts, item_lists, plays, user_factors, item_factors)
    return new_factors, norms.reshape(ITERS + 1)


def solution(mesh):
    split = Mesh(mesh.devices.reshape(NX, NZ, NY, NR), BLK_REP)
    in_specs = (P(BLK, None), P(BLK_REP, None), P(BLK_REP, None), P(BLK_REP), P(BLK_REP, None))
    out_specs = (P(BLK_REP, None), P())
    return jax.shard_map(body, mesh=split, in_specs=in_specs, out_specs=out_specs, check_vma=False)
```

time: 52 us -> 49 us (0.942)
  Pallas kernels: 49.4 us -> 46.4 us
    pallas_call x1, Pallas kernels: 49.4 us -> 46.4 us  [body(): pl.pallas_call(kernel, out_shape=(jax.ShapeDtypeStruct((U, K), F32), jax....]
where the time goes in v2:
time: 49 us; the launch traced here: 48.9 us
  Pallas kernels  46.4 us (95%)
  local copies, waits for them, and re-layouts  1.81 us (4%)
  between operations  0.65 us (1%)
    pallas_call x1, Pallas kernels, body(): pl.pallas_call(kernel, out_shape=(jax.ShapeDtypeStruct((U, K), F32), jax....  46.4 us
    unnamed x4, local copies, waits for them, and re-layouts  1.81 us

profile of v2, /device:TPU:1, one launch (start us, length us, event | category | flops | bytes accessed | tf_op | source)
XLA Modules:
  0.0 48.9 jit_solution(3272814680866322288)
XLA Ops:
  0.6 46.4 %shard_map.68 = (f32[8,256]{1,0:T(8,128)}, f32[1,4]{1,0:T(1,128)}) custom-call(s32[8]{0:T(128)} %counts_hbm.1, s32[8,128]{1,0:T(8,128)} %lists_hbm.1, s32[8,128]{1,0:T(8,128)} %plays_hbm.1, f32[8,256]{1,0:T(8,128)} %users_hbm.1, bf16[2048,256]{1,0:T(8,128)(2,1)} %items_hbm.1), custom_call_target="tpu_custom_call" | custom-call | tf_op jit(solution)/shard_map/pallas_call | solution.py:334
  47.0 0.0 copy-start
  47.0 1.3 %copy.9 = f32[8,256]{1,0:T(8,128)} copy(f32[8,256]{1,0:T(8,128)} %get-tuple-element.8) | data formatting | bytes 16384
  48.3 0.0 copy-done
  48.3 0.5 %copy.10 = f32[4]{0:T(128)} copy(f32[4]{0:T(128)S(1)} %bitcast.1) | data formatting | bytes 32
Async XLA Ops:
  47.0 1.3 %copy-start = (f32[1,4]{1,0:T(1,128)S(1)}, f32[1,4]{1,0:T(1,128)}, u32[]{:S(2)}) copy-start(f32[1,4]{1,0:T(1,128)} %get-tuple-element.5) | copy-start | bytes 52

commit v3 on v2

--- a/solution.py
+++ b/solution.py
@@ -68,6 +68,11 @@
 
 
 NEAR = sorted(((dx, dy) for dx in range(NX) for dy in range(NY)), key=lambda d: (min(d[0], NX - d[0]) + min(d[1], NY - d[1]), d))
+EVERY = sorted(
+    ((d, dz) for d in NEAR for dz in range(NZ) if d != (0, 0) or dz),
+    key=lambda o: -(min(o[0][0], NX - o[0][0]) + min(o[0][1], NY - o[0][1]) + min(o[1], NZ - o[1])),
+)
+STEPS = (0, 7, 6, 5, 4, 3, 2, 1)
 FAR_Z = (4, 3, 5, 2, 6, 1, 7, 0)
 
 
@@ -99,9 +104,9 @@
     rows_in,
     rows_mat,
     norm_send,
-    norm_p,
+    norm_pair,
     norm_mid,
-    norm_z,
+    norm_all,
     local_sems,
     req_sems,
     req_recv,
@@ -237,11 +242,14 @@
             pick = jnp.where(column == (iota((2 * NZ * CAP, width), 1) + part * width).astype(F32), 1.0, 0.0).astype(BF16)
             total = total + dot(pick, items[part * width : (part + 1) * width, :])
         rows_send[step] = total.reshape(2 * NZ, CAP, K).astype(BF16)
-        for i in range(2):
-            d = NEAR[2 * step + i]
-            for j, dz in enumerate(FAR_Z):
+        send_rows(step, FAR_Z[:5])
+
+    def send_rows(step, offsets):
+        for dz in offsets:
+            for i in (1, 0):
+                d = NEAR[2 * step + i]
                 dev = ((x - d[0]) & (NX - 1), (z + dz) & (NZ - 1), (y - d[1]) & (NY - 1), r)
-                src = rows_send.at[step, i * NZ + j]
+                src = rows_send.at[step, i * NZ + FAR_Z.index(dz)]
                 dst = rows_in.at[z * NP + p]
                 if d == (0, 0) and dz == 0:
                     pltpu.make_async_copy(src, dst, rows_recv).start()
@@ -255,12 +263,17 @@
         for d, same in peers:
             send(gram_red, gram_full.at[r * NP + p], gram_sems.at[4], gram_sems.at[5], plane_device(d, same))
 
-    for step in range(NP // 2):
+    for n, step in enumerate(STEPS):
         phase("serve%d" % step)
         serve(step)
-        if step == GRAM_AFTER:
+        if n == GRAM_AFTER:
             phase("gram_ag")
             spread_gram()
+    phase("serve_near")
+    for step in STEPS:
+        send_rows(step, FAR_Z[5:7])
+    for step in STEPS:
+        send_rows(step, FAR_Z[7:])
 
     phase("gram_ag_wait")
     wait_bytes(gram_full.at[pl.ds(0, NP * NR - 1)], gram_sems.at[5])
@@ -302,10 +315,9 @@
         collected = collected + jnp.where(lane == t + 1, squares, 0.0)
 
     norm_send[...] = jnp.sum(collected, axis=0, keepdims=True)
-    phase("norm_p")
-    norm_p[p * NR + r] = norm_send[...]
-    for d, same in peers:
-        send(norm_send, norm_p.at[p * NR + r], norm_sems.at[0], norm_sems.at[1], plane_device(d, same))
+    phase("norm_pair")
+    norm_pair[r] = norm_send[...]
+    send(norm_send, norm_pair.at[r], norm_sems.at[0], norm_sems.at[1], plane_device((0, 0), 0))
     out_ref[...] = solution
     wait_bytes(req_z.at[pl.ds(0, NZ - 1)], req_sems.at[0])
     wait_bytes(req_p.at[pl.ds(0, NP - 1)], req_sems.at[2])
@@ -313,18 +325,19 @@
     wait_bytes(gram_z.at[pl.ds(0, NZ - 1)], gram_sems.at[2])
     wait_bytes(gram_full.at[pl.ds(0, NP * NR - 1)], gram_sems.at[4])
     wait_bytes(rows_in.at[pl.ds(0, NH - 1)], rows_sem)
-    wait_bytes(norm_p.at[pl.ds(0, NP * NR - 1)], norm_sems.at[1])
-    norm_mid[...] = jnp.sum(norm_p[...], axis=0)
-    phase("norm_z")
-    norm_z[z] = norm_mid[...]
-    for dz in FAR_Z[:-1]:
-        send(norm_mid, norm_z.at[z], norm_sems.at[2], norm_sems.at[3], z_device(dz))
-    wait_bytes(norm_p.at[pl.ds(0, NP * NR - 1)], norm_sems.at[0])
-    wait_bytes(norm_z.at[pl.ds(0, NZ - 1)], norm_sems.at[3])
+    wait_bytes(norm_pair.at[pl.ds(0, 1)], norm_sems.at[1])
+    norm_mid[...] = norm_pair[0] + norm_pair[1]
+    phase("norm_all")
+    norm_all[z * NP + p] = norm_mid[...]
+    for d, dz in EVERY:
+        dev = ((x + d[0]) & (NX - 1), (z + dz) & (NZ - 1), (y + d[1]) & (NY - 1), r)
+        send(norm_mid, norm_all.at[z * NP + p], norm_sems.at[2], norm_sems.at[3], dev)
+    wait_bytes(norm_pair.at[pl.ds(0, 1)], norm_sems.at[0])
+    wait_bytes(norm_all.at[pl.ds(0, NH - 1)], norm_sems.at[3])
     phase("norm_end")
-    total = jnp.sum(norm_z[...], axis=0)
+    total = jnp.sum(norm_all[...], axis=0)
     norms_ref[...] = jnp.sqrt(total / (USERS * K))[:, : ITERS + 1]
-    wait_bytes(norm_z.at[pl.ds(0, NZ - 1)], norm_sems.at[2])
+    wait_bytes(norm_all.at[pl.ds(0, NH - 1)], norm_sems.at[2])
     phase(None)
 
 
@@ -333,8 +346,8 @@
     dma = pltpu.SemaphoreType.DMA
     new_factors, norms = pl.pallas_call(
         kernel,
-        out_shape=(jax.ShapeDtypeStruct((U, K), F32), jax.ShapeDtypeStruct((1, ITERS + 1), F32)),
-        in_specs=[pl.BlockSpec(memory_space=pl.ANY)] * 5,
+        out_shape=(pltpu.VMEM((U, K), F32), pltpu.VMEM((1, ITERS + 1), F32)),
+        in_specs=[pl.BlockSpec(memory_space=pltpu.HBM)] * 5,
         out_specs=(vmem, vmem),
         scratch_shapes=[
             pltpu.SMEM((U,), I32),
@@ -357,9 +370,9 @@
             pltpu.VMEM((NH, CAP, K), BF16),
             pltpu.VMEM((NH * CAP, K), BF16),
             pltpu.VMEM((1, L), F32),
-            pltpu.VMEM((NP * NR, 1, L), F32),
+            pltpu.VMEM((NR, 1, L), F32),
             pltpu.VMEM((1, L), F32),
-            pltpu.VMEM((NZ, 1, L), F32),
+            pltpu.VMEM((NH, 1, L), F32),
             dma((5,)),
             dma((3,)),
             dma((NP,)),

time: 49 us -> 45.7 us (0.933)
  Pallas kernels: 46.4 us -> 43.9 us
  local copies, waits for them, and re-layouts: 1.81 us -> 1.11 us
    pallas_call x1, Pallas kernels: 46.4 us -> 43.9 us  [body(): pl.pallas_call(kernel, out_shape=(pltpu.VMEM((U, K), F32), pltpu.VMEM((1,...]
    unnamed x4 -> x2, local copies, waits for them, and re-layouts: 1.81 us -> 1.11 us
where the time goes in v3:
time: 45.7 us; the launch traced here: 45.6 us
  Pallas kernels  43.9 us (96%)
  local copies, waits for them, and re-layouts  1.11 us (2%)
  between operations  0.64 us (1%)
    pallas_call x1, Pallas kernels, body(): pl.pallas_call(kernel, out_shape=(pltpu.VMEM((U, K), F32), pltpu.VMEM((1,...  43.9 us
    unnamed x2, local copies, waits for them, and re-layouts  1.11 us

profile of v3, /device:TPU:1, one launch (start us, length us, event | category | flops | bytes accessed | tf_op | source)
XLA Modules:
  0.0 45.6 jit_solution(17109550731750253142)
XLA Ops:
  0.6 43.9 %shard_map.68 = (f32[8,256]{1,0:T(8,128)S(1)}, f32[1,4]{1,0:T(1,128)S(1)}) custom-call(s32[8]{0:T(128)} %counts_hbm.1, s32[8,128]{1,0:T(8,128)} %lists_hbm.1, s32[8,128]{1,0:T(8,128)} %plays_hbm.1, f32[8,256]{1,0:T(8,128)} %users_hbm.1, bf16[2048,256]{1,0:T(8,128)(2,1)} %items_hbm.1), custom_call_target="tpu_custom_call" | custom-call | tf_op jit(solution)/shard_map/pallas_call | solution.py:347
  44.5 0.6 %copy.9 = f32[8,256]{1,0:T(8,128)} copy(f32[8,256]{1,0:T(8,128)S(1)} %get-tuple-element.6) | data formatting | bytes 16384
  45.1 0.5 %copy.10 = f32[4]{0:T(128)} copy(f32[4]{0:T(128)S(1)} %bitcast.1) | data formatting | bytes 32

commit v4 on v3

--- a/solution.py
+++ b/solution.py
@@ -18,7 +18,7 @@
 U, L, K = 8, 128, 256
 ROWS = 2048
 USERS = U * NH * NR
-GRAM_AFTER = 2
+EXCHANGE_AFTER, SPREAD_AFTER = 0, 5
 F32, BF16, I32 = jnp.float32, jnp.bfloat16, jnp.int32
 
 conf_scale = 40.0
@@ -72,7 +72,7 @@
     ((d, dz) for d in NEAR for dz in range(NZ) if d != (0, 0) or dz),
     key=lambda o: -(min(o[0][0], NX - o[0][0]) + min(o[0][1], NY - o[0][1]) + min(o[1], NZ - o[1])),
 )
-STEPS = (0, 7, 6, 5, 4, 3, 2, 1)
+TILES = (range(0,1),range(1,2),range(2,3),range(3,4),range(4,5), range(5,8), range(14,16), range(11, 14), range(8, 11))
 FAR_Z = (4, 3, 5, 2, 6, 1, 7, 0)
 
 
@@ -102,7 +102,6 @@
     gram3,
     rows_send,
     rows_in,
-    rows_mat,
     norm_send,
     norm_pair,
     norm_mid,
@@ -222,39 +221,12 @@
         dev = plane_device(NEAR[k])
         send(req_fwd.at[place_of(dev)], req_p.at[k], req_sems.at[2], req_recv.at[k], dev)
 
-    phase("gram_p_wait")
-    wait_bytes(gram_p.at[pl.ds(0, NP - 1)], gram_sems.at[1])
-    gram_zsend[...] = jnp.sum(gram_p[...], axis=0)
-    gram_z[z] = gram_zsend[...]
-    for dz in FAR_Z[:-1]:
-        send(gram_zsend, gram_z.at[z], gram_sems.at[2], gram_sems.at[3], z_device(dz))
-
-    def serve(step):
-        tiles = []
-        for k in (2 * step, 2 * step + 1):
-            if k:
-                wait_bytes(req_p.at[k], req_recv.at[k])
-            tiles.append(req_p[k] if k else req_fwd[p])
-        column = jnp.concatenate([t[:, dz : dz + 1] for t in tiles for dz in FAR_Z], axis=0)
-        total = jnp.zeros((2 * NZ * CAP, K), F32)
-        width = 512
-        for part in range(ROWS // width):
-            pick = jnp.where(column == (iota((2 * NZ * CAP, width), 1) + part * width).astype(F32), 1.0, 0.0).astype(BF16)
-            total = total + dot(pick, items[part * width : (part + 1) * width, :])
-        rows_send[step] = total.reshape(2 * NZ, CAP, K).astype(BF16)
-        send_rows(step, FAR_Z[:5])
-
-    def send_rows(step, offsets):
-        for dz in offsets:
-            for i in (1, 0):
-                d = NEAR[2 * step + i]
-                dev = ((x - d[0]) & (NX - 1), (z + dz) & (NZ - 1), (y - d[1]) & (NY - 1), r)
-                src = rows_send.at[step, i * NZ + FAR_Z.index(dz)]
-                dst = rows_in.at[z * NP + p]
-                if d == (0, 0) and dz == 0:
-                    pltpu.make_async_copy(src, dst, rows_recv).start()
-                else:
-                    send(src, dst, rows_sem, rows_recv, dev)
+    def exchange_gram():
+        wait_bytes(gram_p.at[pl.ds(0, NP - 1)], gram_sems.at[1])
+        gram_zsend[...] = jnp.sum(gram_p[...], axis=0)
+        gram_z[z] = gram_zsend[...]
+        for dz in FAR_Z[:-1]:
+            send(gram_zsend, gram_z.at[z], gram_sems.at[2], gram_sems.at[3], z_device(dz))
 
     def spread_gram():
         wait_bytes(gram_z.at[pl.ds(0, NZ - 1)], gram_sems.at[3])
@@ -263,17 +235,39 @@
         for d, same in peers:
             send(gram_red, gram_full.at[r * NP + p], gram_sems.at[4], gram_sems.at[5], plane_device(d, same))
 
-    for n, step in enumerate(STEPS):
-        phase("serve%d" % step)
-        serve(step)
-        if n == GRAM_AFTER:
+    def serve(tiles):
+        for k in tiles:
+            if k:
+                wait_bytes(req_p.at[k], req_recv.at[k])
+        asked = [req_p[k] if k else req_fwd[p] for k in tiles]
+        column = jnp.concatenate([t[:, dz : dz + 1] for t in asked for dz in FAR_Z], axis=0)
+        count = len(tiles) * NZ * CAP
+        total = jnp.zeros((count, K), F32)
+        width = 512
+        for part in range(ROWS // width):
+            pick = jnp.where(column == (iota((count, width), 1) + part * width).astype(F32), 1.0, 0.0).astype(BF16)
+            total = total + dot(pick, items[part * width : (part + 1) * width, :])
+        rows_send[tiles[0] * NZ : (tiles[-1] + 1) * NZ] = total.reshape(len(tiles) * NZ, CAP, K).astype(BF16)
+        for j, dz in enumerate(FAR_Z):
+            for k in reversed(tiles):
+                d = NEAR[k]
+                dev = ((x - d[0]) & (NX - 1), (z + dz) & (NZ - 1), (y - d[1]) & (NY - 1), r)
+                src = rows_send.at[k * NZ + j]
+                dst = rows_in.at[pl.ds(pl.multiple_of((z * NP + p) * CAP, CAP), CAP), :]
+                if k == 0 and dz == 0:
+                    pltpu.make_async_copy(src, dst, rows_recv).start()
+                else:
+                    send(src, dst, rows_sem, rows_recv, dev)
+
+    for n, tiles in enumerate(TILES):
+        phase("serve%d" % n)
+        serve(tiles)
+        if n == EXCHANGE_AFTER:
+            phase("gram_z")
+            exchange_gram()
+        if n == SPREAD_AFTER:
             phase("gram_ag")
             spread_gram()
-    phase("serve_near")
-    for step in STEPS:
-        send_rows(step, FAR_Z[5:7])
-    for step in STEPS:
-        send_rows(step, FAR_Z[7:])
 
     phase("gram_ag_wait")
     wait_bytes(gram_full.at[pl.ds(0, NP * NR - 1)], gram_sems.at[5])
@@ -283,20 +277,19 @@
 
     phase("rows_wait")
     wait_bytes(rows_in, rows_recv)
-    rows_mat[...] = rows_in[...].astype(F32).reshape(NH * CAP, K).astype(BF16)
 
     phase("cg")
     def image_of(v):
         v3 = stacked(v)
-        along = folded(dot_nt(v3, rows_mat[...]), U)
-        back = folded(dot(stacked(extra * along), rows_mat[...]), U)
+        along = folded(dot_nt(v3, rows_in[...]), U)
+        back = folded(dot(stacked(extra * along), rows_in[...]), U)
         g = folded(dot(v3, gram3[...]), U)
         return g[:, :K] + g[:, K : 2 * K] + g[:, 2 * K :] + back + ridge * v
 
     def inner(a, b):
         return jnp.sum(a * b, axis=1, keepdims=True)
 
-    target = folded(dot(stacked(weight), rows_mat[...]), U)
+    target = folded(dot(stacked(weight), rows_in[...]), U)
     copies[3].wait()
     solution = users_ref[...]
     residual = target - image_of(solution)
@@ -324,13 +317,13 @@
     wait_bytes(gram_mine.at[pl.ds(0, NP - 1)], gram_sems.at[0])
     wait_bytes(gram_z.at[pl.ds(0, NZ - 1)], gram_sems.at[2])
     wait_bytes(gram_full.at[pl.ds(0, NP * NR - 1)], gram_sems.at[4])
-    wait_bytes(rows_in.at[pl.ds(0, NH - 1)], rows_sem)
+    wait_bytes(rows_send.at[pl.ds(0, NH - 1)], rows_sem)
     wait_bytes(norm_pair.at[pl.ds(0, 1)], norm_sems.at[1])
     norm_mid[...] = norm_pair[0] + norm_pair[1]
     phase("norm_all")
     norm_all[z * NP + p] = norm_mid[...]
     for d, dz in EVERY:
-        dev = ((x + d[0]) & (NX - 1), (z + dz) & (NZ - 1), (y + d[1]) & (NY - 1), r)
+        dev = ((x + d[0]) & (NX - 1), (z + dz) & (NZ - 1), (y + d[1]) & (NY - 1), 1 - r)
         send(norm_mid, norm_all.at[z * NP + p], norm_sems.at[2], norm_sems.at[3], dev)
     wait_bytes(norm_pair.at[pl.ds(0, 1)], norm_sems.at[0])
     wait_bytes(norm_all.at[pl.ds(0, NH - 1)], norm_sems.at[3])
@@ -366,8 +359,7 @@
             pltpu.VMEM((8, K), F32),
             pltpu.VMEM((NR * NP, 8, K), F32),
             pltpu.VMEM((K, 3 * K), BF16),
-            pltpu.VMEM((NP // 2, 2 * NZ, CAP, K), BF16),
-            pltpu.VMEM((NH, CAP, K), BF16),
+            pltpu.VMEM((NP * NZ, CAP, K), BF16),
             pltpu.VMEM((NH * CAP, K), BF16),
             pltpu.VMEM((1, L), F32),
             pltpu.VMEM((NR, 1, L), F32),

time: 45.7 us -> 44.5 us (0.974)
  Pallas kernels: 43.9 us -> 42.6 us
    pallas_call x1, Pallas kernels: 43.9 us -> 42.6 us  [body(): pl.pallas_call(kernel, out_shape=(pltpu.VMEM((U, K), F32), pltpu.VMEM((1,...]
where the time goes in v4:
time: 44.5 us; the launch traced here: 44.4 us
  Pallas kernels  42.6 us (96%)
  local copies, waits for them, and re-layouts  1.11 us (2%)
  between operations  0.64 us (1%)
    pallas_call x1, Pallas kernels, body(): pl.pallas_call(kernel, out_shape=(pltpu.VMEM((U, K), F32), pltpu.VMEM((1,...  42.6 us
    unnamed x2, local copies, waits for them, and re-layouts  1.11 us

profile of v4, /device:TPU:1, one launch (start us, length us, event | category | flops | bytes accessed | tf_op | source)
XLA Modules:
  0.0 44.4 jit_solution(3484646538527402851)
XLA Ops:
  0.6 42.6 %shard_map.68 = (f32[8,256]{1,0:T(8,128)S(1)}, f32[1,4]{1,0:T(1,128)S(1)}) custom-call(s32[8]{0:T(128)} %counts_hbm.1, s32[8,128]{1,0:T(8,128)} %lists_hbm.1, s32[8,128]{1,0:T(8,128)} %plays_hbm.1, f32[8,256]{1,0:T(8,128)} %users_hbm.1, bf16[2048,256]{1,0:T(8,128)(2,1)} %items_hbm.1), custom_call_target="tpu_custom_call" | custom-call | tf_op jit(solution)/shard_map/pallas_call | solution.py:340
  43.3 0.6 %copy.9 = f32[8,256]{1,0:T(8,128)} copy(f32[8,256]{1,0:T(8,128)S(1)} %get-tuple-element.6) | data formatting | bytes 16384
  43.9 0.5 %copy.10 = f32[4]{0:T(128)} copy(f32[4]{0:T(128)S(1)} %bitcast.1) | data formatting | bytes 32

commit v5 on v4

--- a/solution.py
+++ b/solution.py
@@ -275,6 +275,16 @@
     for k, piece in enumerate(pieces(gram_full[...].reshape(K, K))):
         gram3[:, k * K : (k + 1) * K] = piece
 
+    def gram_part(v3):
+        g = folded(dot(v3, gram3[...]), U)
+        return g[:, :K] + g[:, K : 2 * K] + g[:, 2 * K :]
+
+    copies[3].wait()
+    start = users_ref[...]
+    start3 = stacked(start)
+    start_image = gram_part(start3) + ridge * start
+    weight3 = stacked(weight)
+
     phase("rows_wait")
     wait_bytes(rows_in, rows_recv)
 
@@ -283,16 +293,15 @@
         v3 = stacked(v)
         along = folded(dot_nt(v3, rows_in[...]), U)
         back = folded(dot(stacked(extra * along), rows_in[...]), U)
-        g = folded(dot(v3, gram3[...]), U)
-        return g[:, :K] + g[:, K : 2 * K] + g[:, 2 * K :] + back + ridge * v
+        return gram_part(v3) + back + ridge * v
 
     def inner(a, b):
         return jnp.sum(a * b, axis=1, keepdims=True)
 
-    target = folded(dot(stacked(weight), rows_in[...]), U)
-    copies[3].wait()
-    solution = users_ref[...]
-    residual = target - image_of(solution)
+    along = folded(dot_nt(start3, rows_in[...]), U)
+    both = dot(jnp.concatenate([weight3.astype(F32), stacked(extra * along).astype(F32)], axis=0).astype(BF16), rows_in[...])
+    solution = start
+    residual = folded(both[: 3 * U], U) - (start_image + folded(both[3 * U :], U))
     direction = residual
     squares = inner(residual, residual)
     lane = iota((U, L), 1)
@@ -332,6 +341,14 @@
     norms_ref[...] = jnp.sqrt(total / (USERS * K))[:, : ITERS + 1]
     wait_bytes(norm_all.at[pl.ds(0, NH - 1)], norm_sems.at[2])
     phase(None)
+
+
+def put_out(factors, norms, factors_out, norms_out, sems):
+    copies = [pltpu.make_async_copy(factors, factors_out, sems.at[0]), pltpu.make_async_copy(norms, norms_out, sems.at[1])]
+    for copy in copies:
+        copy.start()
+    for copy in copies:
+        copy.wait()
 
 
 def body(item_factors, user_factors, item_lists, counts, plays):
@@ -375,6 +392,14 @@
         ],
         compiler_params=pltpu.CompilerParams(collective_id=0, has_side_effects=True),
     )(counts, item_lists, plays, user_factors, item_factors)
+    new_factors, norms = pl.pallas_call(
+        put_out,
+        out_shape=(jax.ShapeDtypeStruct((U, K), F32), jax.ShapeDtypeStruct((1, ITERS + 1), F32)),
+        in_specs=[vmem, vmem],
+        out_specs=(pl.BlockSpec(memory_space=pltpu.HBM), pl.BlockSpec(memory_space=pltpu.HBM)),
+        scratch_shapes=[dma((2,))],
+        compiler_params=pltpu.CompilerParams(vmem_limit_bytes=1024 * 1024),
+    )(new_factors, norms)
     return new_factors, norms.reshape(ITERS + 1)
 
 

time: 44.5 us -> 43.7 us (0.982)
  local copies, waits for them, and re-layouts: 1.11 us -> 0 us
    unnamed x2 -> x0, local copies, waits for them, and re-layouts: 1.11 us -> none
    pallas_call x0 -> x1, Pallas kernels: none -> 0.62 us  [body(): pl.pallas_call(put_out, out_shape=(jax.ShapeDtypeStruct((U, K), F32), jax...]
where the time goes in v5:
time: 43.7 us; the launch traced here: 43.6 us
  Pallas kernels  43 us (98%)
  between operations  0.64 us (1%)
    pallas_call x1, Pallas kernels, body(): pl.pallas_call(kernel, out_shape=(pltpu.VMEM((U, K), F32), pltpu.VMEM((1,...  42.4 us

profile of v5, /device:TPU:1, one launch (start us, length us, event | category | flops | bytes accessed | tf_op | source)
XLA Modules:
  0.0 43.6 jit_solution(1045182587391674468)
XLA Ops:
  0.6 42.4 %shard_map.68 = (f32[8,256]{1,0:T(8,128)S(1)}, f32[1,4]{1,0:T(1,128)S(1)}) custom-call(s32[8]{0:T(128)} %counts_hbm.1, s32[8,128]{1,0:T(8,128)} %lists_hbm.1, s32[8,128]{1,0:T(8,128)} %plays_hbm.1, f32[8,256]{1,0:T(8,128)} %users_hbm.1, bf16[2048,256]{1,0:T(8,128)(2,1)} %items_hbm.1), custom_call_target="tpu_custom_call" | custom-call | tf_op jit(solution)/shard_map/pallas_call | solution.py:357
  43.0 0.6 %shard_map.69 = (f32[8,256]{1,0:T(8,128)}, f32[1,4]{1,0:T(1,128)}) custom-call(f32[8,256]{1,0:T(8,128)S(1)} %get-tuple-element.6.factors, f32[1,4]{1,0:T(1,128)S(1)} %get-tuple-element.7.norms), custom_call_target="tpu_custom_call" | custom-call | tf_op jit(solution)/shard_map/pallas_call | solution.py:395

commit v6 on v5

--- a/solution.py
+++ b/solution.py
@@ -18,7 +18,7 @@
 U, L, K = 8, 128, 256
 ROWS = 2048
 USERS = U * NH * NR
-EXCHANGE_AFTER, SPREAD_AFTER = 0, 5
+EXCHANGE_AFTER, SPREAD_AFTER = 0, 4
 F32, BF16, I32 = jnp.float32, jnp.bfloat16, jnp.int32
 
 conf_scale = 40.0
@@ -72,8 +72,23 @@
     ((d, dz) for d in NEAR for dz in range(NZ) if d != (0, 0) or dz),
     key=lambda o: -(min(o[0][0], NX - o[0][0]) + min(o[0][1], NY - o[0][1]) + min(o[1], NZ - o[1])),
 )
-TILES = (range(0,1),range(1,2),range(2,3),range(3,4),range(4,5), range(5,8), range(14,16), range(11, 14), range(8, 11))
+DIRECT = range(1, 5)
+DIRECT_Z = (3, 5, 2, 6, 1, 7, 0)
+GROUPS = (
+    [(0, dz) for dz in (4, 3, 5, 2, 6, 1, 7, 0)],
+    [(k, dz) for dz in DIRECT_Z for k in DIRECT],
+    *([(k, dz) for dz in (4, 3, 5, 2, 6, 1, 7, 0) for k in (*more, *tiles) if dz == 4 or k in tiles]
+      for tiles, more in ((range(5, 8), DIRECT), (range(14, 16), ()), (range(11, 14), ()), (range(8, 11), ()))),
+)
 FAR_Z = (4, 3, 5, 2, 6, 1, 7, 0)
+
+
+def hops(d, dz):
+    return min(d[0], NX - d[0]) + min(d[1], NY - d[1]) + min(dz, NZ - dz)
+
+
+def direct_slot(k, dz):
+    return (k - DIRECT[0]) * len(DIRECT_Z) + DIRECT_Z.index(dz)
 
 
 def kernel(
@@ -91,6 +106,8 @@
     items,
     req_send,
     req_z,
+    req_near,
+    req_near_t,
     req_fwd,
     req_p,
     gram_mine,
@@ -108,6 +125,7 @@
     norm_all,
     local_sems,
     req_sems,
+    req_near_recv,
     req_recv,
     gram_sems,
     rows_sem,
@@ -122,6 +140,9 @@
     def plane_device(d, same=1):
         return ((x + d[0]) & (NX - 1), z, (y + d[1]) & (NY - 1), r if same else 1 - r)
 
+    def device(d, dz):
+        return ((x + d[0]) & (NX - 1), (z + dz) & (NZ - 1), (y + d[1]) & (NY - 1), r)
+
     def z_device(dz):
         return (x, (z + dz) & (NZ - 1), y, r)
 
@@ -147,10 +168,11 @@
     for copy in copies:
         copy.start()
     barrier = pltpu.get_barrier_semaphore()
-    for dz in range(1, NZ):
-        pl.semaphore_signal(barrier, inc=1, device_id=z_device(dz), device_id_type=MESH)
-    for d, same in peers:
-        pl.semaphore_signal(barrier, inc=1, device_id=plane_device(d, same), device_id_type=MESH)
+    greeted = [((0, 0), dz, 1) for dz in range(1, NZ)] + [(d, 0, same) for d, same in peers]
+    greeted += [(NEAR[k], dz, 1) for k in DIRECT for dz in DIRECT_Z[:-1]]
+    for d, dz, same in sorted(greeted, key=lambda o: -hops(o[0], o[1])):
+        dev = (*device(d, dz)[:3], r if same else 1 - r)
+        pl.semaphore_signal(barrier, inc=1, device_id=dev, device_id_type=MESH)
     for copy in copies[:3]:
         copy.wait()
 
@@ -197,10 +219,15 @@
     req_z[0] = req_send[z]
 
     phase("barrier")
-    pl.semaphore_wait(barrier, NP * NR - 1 + NZ - 1)
+    pl.semaphore_wait(barrier, len(greeted))
     for dz in FAR_Z[:-1]:
         dev = z_device(dz)
         send(req_send.at[dev[1]], req_z.at[NZ - dz], req_sems.at[0], req_sems.at[1], dev)
+    for dz in DIRECT_Z:
+        for k in DIRECT:
+            dev = device(NEAR[k], dz)
+            at = direct_slot(k, (NZ - dz) % NZ)
+            send(req_send.at[dev[1]], req_near.at[at], req_sems.at[0], req_near_recv, dev)
 
     phase("gram")
     copies[4].wait()
@@ -235,33 +262,45 @@
         for d, same in peers:
             send(gram_red, gram_full.at[r * NP + p], gram_sems.at[4], gram_sems.at[5], plane_device(d, same))
 
-    def serve(tiles):
-        for k in tiles:
-            if k:
-                wait_bytes(req_p.at[k], req_recv.at[k])
-        asked = [req_p[k] if k else req_fwd[p] for k in tiles]
-        column = jnp.concatenate([t[:, dz : dz + 1] for t in asked for dz in FAR_Z], axis=0)
-        count = len(tiles) * NZ * CAP
+    def serve(first, goals):
+        direct = goals is GROUPS[1]
+        if direct:
+            wait_bytes(req_near, req_near_recv)
+            known = len(DIRECT) * len(DIRECT_Z)
+            near = jnp.concatenate([req_near[...].reshape(known, L), jnp.zeros((L - known, L), F32)], axis=0).T
+            req_near_t[...] = near.reshape(NP, CAP, L)
+            near = req_near_t[p]
+            columns = [near[:, direct_slot(k, dz) : direct_slot(k, dz) + 1] for k, dz in goals]
+        else:
+            tiles = {}
+            for k in sorted({k for k, _ in goals}):
+                if k:
+                    wait_bytes(req_p.at[k], req_recv.at[k])
+                tiles[k] = req_p[k] if k else req_fwd[p]
+            columns = [tiles[k][:, dz : dz + 1] for k, dz in goals]
+        column = jnp.concatenate(columns, axis=0)
+        count = len(goals) * CAP
         total = jnp.zeros((count, K), F32)
         width = 512
         for part in range(ROWS // width):
             pick = jnp.where(column == (iota((count, width), 1) + part * width).astype(F32), 1.0, 0.0).astype(BF16)
             total = total + dot(pick, items[part * width : (part + 1) * width, :])
-        rows_send[tiles[0] * NZ : (tiles[-1] + 1) * NZ] = total.reshape(len(tiles) * NZ, CAP, K).astype(BF16)
-        for j, dz in enumerate(FAR_Z):
-            for k in reversed(tiles):
-                d = NEAR[k]
-                dev = ((x - d[0]) & (NX - 1), (z + dz) & (NZ - 1), (y - d[1]) & (NY - 1), r)
-                src = rows_send.at[k * NZ + j]
-                dst = rows_in.at[pl.ds(pl.multiple_of((z * NP + p) * CAP, CAP), CAP), :]
-                if k == 0 and dz == 0:
-                    pltpu.make_async_copy(src, dst, rows_recv).start()
-                else:
-                    send(src, dst, rows_sem, rows_recv, dev)
-
-    for n, tiles in enumerate(TILES):
+        rows_send[first : first + len(goals)] = total.reshape(len(goals), CAP, K).astype(BF16)
+        for i, (k, dz) in enumerate(goals):
+            d = NEAR[k]
+            dev = ((x - d[0]) & (NX - 1), (z + dz) & (NZ - 1), (y - d[1]) & (NY - 1), r)
+            src = rows_send.at[first + i]
+            dst = rows_in.at[pl.ds(pl.multiple_of((z * NP + p) * CAP, CAP), CAP), :]
+            if k == 0 and dz == 0:
+                pltpu.make_async_copy(src, dst, rows_recv).start()
+            else:
+                send(src, dst, rows_sem, rows_recv, dev)
+        return first + len(goals)
+
+    served = 0
+    for n, goals in enumerate(GROUPS):
         phase("serve%d" % n)
-        serve(tiles)
+        served = serve(served, goals)
         if n == EXCHANGE_AFTER:
             phase("gram_z")
             exchange_gram()
@@ -322,6 +361,7 @@
     send(norm_send, norm_pair.at[r], norm_sems.at[0], norm_sems.at[1], plane_device((0, 0), 0))
     out_ref[...] = solution
     wait_bytes(req_z.at[pl.ds(0, NZ - 1)], req_sems.at[0])
+    wait_bytes(req_near, req_sems.at[0])
     wait_bytes(req_p.at[pl.ds(0, NP - 1)], req_sems.at[2])
     wait_bytes(gram_mine.at[pl.ds(0, NP - 1)], gram_sems.at[0])
     wait_bytes(gram_z.at[pl.ds(0, NZ - 1)], gram_sems.at[2])
@@ -367,6 +407,8 @@
             pltpu.VMEM((ROWS, K), BF16),
             pltpu.VMEM((NZ, 1, L), F32),
             pltpu.VMEM((NZ, 1, L), F32),
+            pltpu.VMEM((len(DIRECT) * len(DIRECT_Z), 1, L), F32),
+            pltpu.VMEM((NP, CAP, L), F32),
             pltpu.VMEM((NP, CAP, L), F32),
             pltpu.VMEM((NP, CAP, L), F32),
             pltpu.VMEM((NP, 8, K), F32),
@@ -384,6 +426,7 @@
             pltpu.VMEM((NH, 1, L), F32),
             dma((5,)),
             dma((3,)),
+            dma,
             dma((NP,)),
             dma((6,)),
             dma,

time: 43.7 us -> 43.1 us (0.986)
  Pallas kernels: 43 us -> 42.4 us
    pallas_call x1, Pallas kernels: 42.4 us -> 41.7 us  [body(): pl.pallas_call(kernel, out_shape=(pltpu.VMEM((U, K), F32), pltpu.VMEM((1,...]
where the time goes in v6:
time: 43.1 us; the launch traced here: 43 us
  Pallas kernels  42.4 us (98%)
  between operations  0.64 us (1%)
    pallas_call x1, Pallas kernels, body(): pl.pallas_call(kernel, out_shape=(pltpu.VMEM((U, K), F32), pltpu.VMEM((1,...  41.7 us

profile of v6, /device:TPU:1, one launch (start us, length us, event | category | flops | bytes accessed | tf_op | source)
XLA Modules:
  0.0 43.0 jit_solution(3082614398240713311)
XLA Ops:
  0.6 41.7 %shard_map.68 = (f32[8,256]{1,0:T(8,128)S(1)}, f32[1,4]{1,0:T(1,128)S(1)}) custom-call(s32[8]{0:T(128)} %counts_hbm.1, s32[8,128]{1,0:T(8,128)} %lists_hbm.1, s32[8,128]{1,0:T(8,128)} %plays_hbm.1, f32[8,256]{1,0:T(8,128)} %users_hbm.1, bf16[2048,256]{1,0:T(8,128)(2,1)} %items_hbm.1), custom_call_target="tpu_custom_call" | custom-call | tf_op jit(solution)/shard_map/pallas_call | solution.py:397
  42.4 0.6 %shard_map.69 = (f32[8,256]{1,0:T(8,128)}, f32[1,4]{1,0:T(1,128)}) custom-call(f32[8,256]{1,0:T(8,128)S(1)} %get-tuple-element.6.factors, f32[1,4]{1,0:T(1,128)S(1)} %get-tuple-element.7.norms), custom_call_target="tpu_custom_call" | custom-call | tf_op jit(solution)/shard_map/pallas_call | solution.py:438

commit v7 on v6

--- a/solution.py
+++ b/solution.py
@@ -119,6 +119,7 @@
     gram3,
     rows_send,
     rows_in,
+    rows_t,
     norm_send,
     norm_pair,
     norm_mid,
@@ -165,14 +166,14 @@
             [(counts_hbm, counts_ref), (lists_hbm, lists_ref), (plays_hbm, plays_ref), (users_hbm, users_ref), (items_hbm, items)]
         )
     ]
-    for copy in copies:
-        copy.start()
     barrier = pltpu.get_barrier_semaphore()
     greeted = [((0, 0), dz, 1) for dz in range(1, NZ)] + [(d, 0, same) for d, same in peers]
     greeted += [(NEAR[k], dz, 1) for k in DIRECT for dz in DIRECT_Z[:-1]]
     for d, dz, same in sorted(greeted, key=lambda o: -hops(o[0], o[1])):
         dev = (*device(d, dz)[:3], r if same else 1 - r)
         pl.semaphore_signal(barrier, inc=1, device_id=dev, device_id_type=MESH)
+    for copy in copies:
+        copy.start()
     for copy in copies[:3]:
         copy.wait()
 
@@ -330,14 +331,15 @@
     phase("cg")
     def image_of(v):
         v3 = stacked(v)
-        along = folded(dot_nt(v3, rows_in[...]), U)
+        along = folded(dot(v3, rows_t[...]), U)
         back = folded(dot(stacked(extra * along), rows_in[...]), U)
         return gram_part(v3) + back + ridge * v
 
     def inner(a, b):
         return jnp.sum(a * b, axis=1, keepdims=True)
 
-    along = folded(dot_nt(start3, rows_in[...]), U)
+    rows_t[...] = rows_in[...].T
+    along = folded(dot(start3, rows_t[...]), U)
     both = dot(jnp.concatenate([weight3.astype(F32), stacked(extra * along).astype(F32)], axis=0).astype(BF16), rows_in[...])
     solution = start
     residual = folded(both[: 3 * U], U) - (start_image + folded(both[3 * U :], U))
@@ -420,6 +422,7 @@
             pltpu.VMEM((K, 3 * K), BF16),
             pltpu.VMEM((NP * NZ, CAP, K), BF16),
             pltpu.VMEM((NH * CAP, K), BF16),
+            pltpu.VMEM((K, NH * CAP), BF16),
             pltpu.VMEM((1, L), F32),
             pltpu.VMEM((NR, 1, L), F32),
             pltpu.VMEM((1, L), F32),

time: 43.1 us -> 43 us (level)
  no operation moved by 1% of the time
where the time goes in v7:
time: 43 us; the launch traced here: 42.9 us
  Pallas kernels  42.3 us (98%)
  between operations  0.64 us (1%)
    pallas_call x1, Pallas kernels, body(): pl.pallas_call(kernel, out_shape=(pltpu.VMEM((U, K), F32), pltpu.VMEM((1,...  41.7 us

profile of v7, /device:TPU:1, one launch (start us, length us, event | category | flops | bytes accessed | tf_op | source)
XLA Modules:
  0.0 42.9 jit_solution(11751813579952305407)
XLA Ops:
  0.6 41.7 %shard_map.68 = (f32[8,256]{1,0:T(8,128)S(1)}, f32[1,4]{1,0:T(1,128)S(1)}) custom-call(s32[8]{0:T(128)} %counts_hbm.1, s32[8,128]{1,0:T(8,128)} %lists_hbm.1, s32[8,128]{1,0:T(8,128)} %plays_hbm.1, f32[8,256]{1,0:T(8,128)} %users_hbm.1, bf16[2048,256]{1,0:T(8,128)(2,1)} %items_hbm.1), custom_call_target="tpu_custom_call" | custom-call | tf_op jit(solution)/shard_map/pallas_call | solution.py:399
  42.3 0.6 %shard_map.69 = (f32[8,256]{1,0:T(8,128)}, f32[1,4]{1,0:T(1,128)}) custom-call(f32[8,256]{1,0:T(8,128)S(1)} %get-tuple-element.6.factors, f32[1,4]{1,0:T(1,128)S(1)} %get-tuple-element.7.norms), custom_call_target="tpu_custom_call" | custom-call | tf_op jit(solution)/shard_map/pallas_call | solution.py:441

commit v8 on v6

--- a/solution.py
+++ b/solution.py
@@ -18,7 +18,7 @@
 U, L, K = 8, 128, 256
 ROWS = 2048
 USERS = U * NH * NR
-EXCHANGE_AFTER, SPREAD_AFTER = 0, 4
+EXCHANGE_AFTER, SPREAD_AFTER = 0, 5
 F32, BF16, I32 = jnp.float32, jnp.bfloat16, jnp.int32
 
 conf_scale = 40.0

time: 43.1 us -> 43.1 us (level)
  no operation moved by 1% of the time
where the time goes in v8:
time: 43.1 us; the launch traced here: 43 us
  Pallas kernels  42.4 us (98%)
  between operations  0.64 us (1%)
    pallas_call x1, Pallas kernels, body(): pl.pallas_call(kernel, out_shape=(pltpu.VMEM((U, K), F32), pltpu.VMEM((1,...  41.7 us

profile of v8, /device:TPU:1, one launch (start us, length us, event | category | flops | bytes accessed | tf_op | source)
XLA Modules:
  0.0 43.0 jit_solution(603355091623585624)
XLA Ops:
  0.6 41.7 %shard_map.68 = (f32[8,256]{1,0:T(8,128)S(1)}, f32[1,4]{1,0:T(1,128)S(1)}) custom-call(s32[8]{0:T(128)} %counts_hbm.1, s32[8,128]{1,0:T(8,128)} %lists_hbm.1, s32[8,128]{1,0:T(8,128)} %plays_hbm.1, f32[8,256]{1,0:T(8,128)} %users_hbm.1, bf16[2048,256]{1,0:T(8,128)(2,1)} %items_hbm.1), custom_call_target="tpu_custom_call" | custom-call | tf_op jit(solution)/shard_map/pallas_call | solution.py:397
  42.4 0.6 %shard_map.69 = (f32[8,256]{1,0:T(8,128)}, f32[1,4]{1,0:T(1,128)}) custom-call(f32[8,256]{1,0:T(8,128)S(1)} %get-tuple-element.6.factors, f32[1,4]{1,0:T(1,128)S(1)} %get-tuple-element.7.norms), custom_call_target="tpu_custom_call" | custom-call | tf_op jit(solution)/shard_map/pallas_call | solution.py:438
